TPU v7x, 512 devices: a whole 4x8x8 slice. The times are simulated.
512 devices in a mesh: ga: 128 (over z, y, core), band: 4 (over x).
Axes of the slice: x: 4, y: 8, z: 8, core: 2. Of those that a mesh axis runs over, the one named last changes fastest.
Arguments:
- coeffs: bfloat16 [32768, 128], P('ga', 'band'), may hold values from -6 to 6
- coupling: bfloat16 [12288, 12288], P('ga', 'band'), may hold values from -0.21875 to 0.21875
- miller: int32 [3, 32768], P(None, 'ga'), may hold values from -24 to 24
- species: int32 [1024], replicated, may hold values from 0 to 3
- proj_atom: int32 [12288], replicated, may hold values from 0 to 1023, as said below
- positions: float32 [3, 1024], replicated, may hold values from 0 to 1
- radial: float32 [12, 128], replicated, may hold values from -8 to 8
Outputs:
- result: bfloat16 [32768, 128], P('ga', 'band')
Inputs may be any that keep to these rules, and one draw needn't show every extreme that they name: `proj_atom`: projector p has channel p mod 12; each atom owns 12 consecutive projectors.
All inputs are finite; a program needn't handle non-finite values.
Results may differ from a plain program's by a relative error of at most 0.008.
Values may be sent and summed in bfloat16 or wider, within the bound.
A program may use at most 64 MiB of HBM per device.

v0:
```python
import math

import jax
import jax.numpy as jnp
from jax import lax
from jax.sharding import Mesh
from jax.sharding import PartitionSpec as P

NCH = 12
SHELLS = 3
KINDS = 4
QBINS = 128
MMAX = 24
NPROJ = 12288
GA = ("ga_0", "ga_1", "ga_2")


def cut_along(array, dim, devices):
    dims = array.shape
    pieces = array.reshape(*dims[:dim], devices, dims[dim] // devices, *dims[dim + 1 :])
    return jnp.moveaxis(pieces, dim, 0)


def summed_on_arrival(array, axis, dim):
    pieces = cut_along(array, dim, lax.axis_size(axis))
    arrived = lax.all_to_all(pieces, axis, split_axis=0, concat_axis=0, tiled=True)
    return arrived.sum(axis=0)


def sum_by_axis(array, axes, dim):
    far, near = axes
    pieces = cut_along(array, dim, lax.axis_size(far))
    nearer = summed_on_arrival(pieces, near, dim + 1)
    arrived = lax.all_to_all(nearer, far, split_axis=0, concat_axis=0, tiled=True)
    return arrived.sum(axis=0)


def padded_to(lines, devices):
    spare = -len(lines) % devices
    return jnp.pad(lines, [(0, spare)] + [(0, 0)] * (lines.ndim - 1))


def from_everyone(array, axis):
    devices = lax.axis_size(axis)
    return lax.all_to_all(
        jnp.broadcast_to(array[None], (devices, *array.shape)), axis, 0, 0, tiled=True
    )


def joined_along(pieces, dim):
    dims = list(pieces.shape[1:])
    dims[dim] *= pieces.shape[0]
    return jnp.moveaxis(pieces, 0, dim).reshape(dims)


def gathered_by_axis(array, axes, dim):
    far, near = axes
    pieces = from_everyone(from_everyone(array, far), near)
    return joined_along(pieces.swapaxes(0, 1).reshape(-1, *array.shape), dim)


def sum_by_parts(array, axes):
    lines = array.reshape(-1)
    own = sum_by_axis(padded_to(lines, lax.axis_size(axes[0]) * lax.axis_size(axes[1])), axes, 0)
    whole = gathered_by_axis(own, axes, 0)
    return whole[: len(lines)].reshape(array.shape)


def collect(array, axis, dim):
    pieces = from_everyone(array, axis)
    return joined_along(pieces, dim)


def radial_values(miller_block, radial):
    mf = miller_block.astype(jnp.float32)
    qval = (mf[0] * mf[0] + mf[1] * mf[1] + mf[2] * mf[2]) * ((QBINS - 1) / (3.0 * MMAX * MMAX))
    knots = jnp.arange(QBINS, dtype=jnp.int32).astype(jnp.float32)
    hats = jnp.maximum(0.0, 1.0 - jnp.abs(qval[:, None] - knots[None, :]))
    return jnp.dot(hats, radial.T, precision=lax.Precision.HIGHEST)


def beta_columns(miller_block, radval, species, proj_atom, positions, start, count, scale):
    mf = miller_block.astype(jnp.float32)
    atoms = lax.dynamic_slice_in_dim(proj_atom, jnp.asarray(start).astype(jnp.int32), count)
    channel = (jnp.asarray(start).astype(jnp.int32) + jnp.arange(count, dtype=jnp.int32)) % NCH
    shell = channel // 4
    comp = channel % 4
    kind = jnp.take(species, atoms)
    column = kind * SHELLS + shell
    select = (column[None, :] == jnp.arange(KINDS * SHELLS, dtype=jnp.int32)[:, None]).astype(
        jnp.float32
    )
    radpart = jnp.dot(radval, select, precision=lax.Precision.HIGHEST)
    place = jnp.take(positions, atoms, axis=1)
    theta = (
        2.0
        * math.pi
        * (
            mf[0][:, None] * place[0][None, :]
            + mf[1][:, None] * place[1][None, :]
            + mf[2][:, None] * place[2][None, :]
        )
    )
    unit = mf / MMAX
    angular = jnp.where(
        comp[None, :] == 1,
        unit[0][:, None],
        jnp.where(
            comp[None, :] == 2,
            unit[1][:, None],
            jnp.where(comp[None, :] == 3, unit[2][:, None], jnp.ones_like(theta)),
        ),
    )
    phase = jnp.where(comp[None, :] == 0, jnp.cos(theta), jnp.sin(theta))
    return (radpart * angular * phase * scale).astype(jnp.bfloat16)


def beta_atoms(miller_block, radval, species, proj_atom, positions, start, count, scale):
    mf = miller_block.astype(jnp.float32)
    npw = mf.shape[1]
    natoms = count // NCH
    owners = lax.dynamic_slice_in_dim(proj_atom, jnp.asarray(start).astype(jnp.int32), count)
    atoms = owners.reshape(natoms, NCH)[:, 0]
    kind = jnp.take(species, atoms)
    column = kind[:, None] * SHELLS + jnp.arange(SHELLS, dtype=jnp.int32)[None, :]
    select = (
        column.reshape(-1)[None, :] == jnp.arange(KINDS * SHELLS, dtype=jnp.int32)[:, None]
    ).astype(jnp.float32)
    radpart = jnp.dot(radval, select, precision=lax.Precision.HIGHEST).reshape(npw, natoms, SHELLS)
    place = jnp.take(positions, atoms, axis=1)
    theta = (
        2.0
        * math.pi
        * (
            mf[0][:, None] * place[0][None, :]
            + mf[1][:, None] * place[1][None, :]
            + mf[2][:, None] * place[2][None, :]
        )
    )
    cosine = jnp.cos(theta)
    sine = jnp.sin(theta)
    unit = mf / MMAX
    ones = jnp.ones((npw, natoms), jnp.float32)
    angular = jnp.stack(
        [
            ones,
            jnp.broadcast_to(unit[0][:, None], (npw, natoms)),
            jnp.broadcast_to(unit[1][:, None], (npw, natoms)),
            jnp.broadcast_to(unit[2][:, None], (npw, natoms)),
        ],
        axis=2,
    )
    phase = jnp.stack([cosine, sine, sine, sine], axis=2)
    values = radpart[:, :, :, None] * angular[:, :, None, :] * phase[:, :, None, :] * scale
    return values.reshape(npw, count).astype(jnp.bfloat16)


def make_beta(miller_block, radval, species, proj_atom, positions, start, count, scale, aligned):
    if aligned and count % NCH == 0:
        return beta_atoms(miller_block, radval, species, proj_atom, positions, start, count, scale)
    return beta_columns(miller_block, radval, species, proj_atom, positions, start, count, scale)


def block_size(count):
    width = 1
    for cand in range(min(count, 768), 0, -1):
        if count % cand == 0:
            width = cand
            break
    return width


def shards(coeffs, coupling, miller, species, proj_atom, positions, radial):
    scale = 1.0 / math.sqrt(coeffs.shape[0] * lax.axis_size(GA))
    radval = radial_values(miller, radial)
    nbands = coeffs.shape[1]
    aligned = coupling.shape[0] % NCH == 0
    width = block_size(NPROJ)
    starts = width * jnp.arange(NPROJ // width, dtype=jnp.int32)

    def one_block(first):
        beta = make_beta(
            miller, radval, species, proj_atom, positions, first, width, scale, aligned
        )
        return lax.dot_general(
            beta, coeffs, (((0,), (0,)), ((), ())), preferred_element_type=jnp.float32
        )

    summed = sum_by_parts(
        lax.map(one_block, starts).reshape(NPROJ, nbands), (("ga_0", "ga_1"), "ga_2")
    )
    proj_b = summed.astype(jnp.bfloat16)
    full_rows = collect(coupling, "band", 1)
    mixed = jnp.dot(full_rows, proj_b, preferred_element_type=jnp.float32).astype(jnp.bfloat16)
    piece = gathered_by_axis(mixed, (("ga_0", "ga_1"), "ga_2"), 0)
    start = jnp.int32(0)
    count = piece.shape[0]
    add_width = block_size(count)

    def step(index, acc):
        first = start + index * add_width
        beta = make_beta(
            miller, radval, species, proj_atom, positions, first, add_width, scale, aligned
        )
        rows = lax.dynamic_slice_in_dim(piece, index * add_width, add_width, 0)
        return acc + jnp.dot(beta, rows, preferred_element_type=jnp.float32)

    summed_back = lax.fori_loop(0, count // add_width, step, coeffs.astype(jnp.float32))
    return summed_back.astype(jnp.bfloat16)


def solution(mesh):
    torus = Mesh(
        mesh.devices.reshape(8, 8, 2, mesh.shape["band"]), ("ga_0", "ga_1", "ga_2", "band")
    )
    return jax.shard_map(
        shards,
        mesh=torus,
        in_specs=(P(GA, "band"), P(GA, "band"), P(None, GA), P(), P(), P(), P()),
        out_specs=P(GA, "band"),
        check_vma=False,
    )
```

profile of v0, /device:TPU:1, one launch (start us, length us, event | category | flops | bytes accessed | tf_op | source)
XLA Modules:
  0.0 408.7 jit_solution(12641493432336062470)
XLA Ops:
  2.0 135.1 %while.27 = (s32[]{:T(128)}, f32[16,768,32]{1,2,0:T(8,128)S(1)}, s32[16]{0:T(128)S(1)}, s32[12288]{0:T(1024)}, s32[1024]{0:T(1024)}, /*index=5*/f32[256,12]{0,1:...) while((s32[]{:T(128)}, f32[16,768,32]{1,2,0:T(8,128)S(1)}, ...), condition=%wide.region_1.4_spmd, body=%wide.region_0.3_spmd.sunk | while | flops 20943940 | bytes 4833151 | solution.py:190
  5.8 1.5 gather_fusion.1
  14.2 1.5 gather_fusion.1
  22.6 1.5 gather_fusion.1
  39.5 1.5 gather_fusion.1
  48.0 1.5 gather_fusion.1
  56.4 1.5 gather_fusion.1
  64.9 1.5 gather_fusion.1
  81.8 1.5 gather_fusion.1
  90.2 1.5 gather_fusion.1
  98.7 1.5 gather_fusion.1
  137.1 4.1 copy.38
  141.2 5.4 %reshape_reshape.7 = f32[64,2,3072]{2,1,0:T(2,128)S(1)} reshape(f32[16,768,32]{2,1,0:T(8,128)} %copy.38) | data formatting | bytes 3145728 | tf_op jit(solution)/shard_map/reshape;reshape | solution.py:20
  147.0 11.5 %all_to_all.40 = f32[2,64,3072]{2,1,0:T(8,128)S(1)} all-to-all(f32[2,64,3072]{2,1,0:T(8,128)S(1)} %copy.39), channel_id=1, replica_groups=mesh['ga_0'=8,'ga_1'=8,'ga_2'=2,'band'=4] {'ga_2'}, dimensions={0} | all-to-all | bytes 3145728 | tf_op jit(solution)/shard_map/all_to_all | solution.py:26
  159.3 33.3 %all_to_all.41 = f32[64,1,3072]{2,1,0:T(1,128)S(1)} all-to-all(f32[64,1,3072]{2,1,0:T(1,128)S(1)} %all_to_all.26), channel_id=1, replica_groups=mesh['ga_0'=8,'ga_1'=8,'ga_2'=2,'band'=4] {'ga_0','ga_1'}, dimensions={0} | all-to-all | bytes 1572864 | tf_op jit(solution)/shard_map/all_to_all | solution.py:34
  192.6 1.7 broadcast_in_dim.148
  194.3 4.0 all-to-all-start.4
  199.9 3.8 reduce.17
  203.8 2.0 reshape.1014
  205.8 19.2 %all-to-all-done.4 = bf16[4,96,3072]{2,1,0:T(8,128)(2,1)S(1)} async-done(((bf16[4,96,3072]{2,1,0:T(8,128)(2,1)}), bf16[4,96,3072]{2,1,0:T(8,128)(2,1)S(1)}, u32[]{:S(2)}, u32[]{:S(2)}) %all-to-all-start.4) | async-done | bytes 2359328 | tf_op jit(solution)/shard_map/all_to_all | solution.py:45
  225.0 8.4 %all-to-all-start.2 = ((bf16[64,2,1536]{2,1,0:T(2,128)(2,1)}), bf16[64,2,1536]{2,1,0:T(2,128)(2,1)S(1)}, u32[]{:S(2)}, u32[]{:S(2)}) async-start(bf16[64,2,1536]{2,1,0:T(2,128)(2,1)} %reshape.1014), calls=%async_computation.2 | async-start | bytes 786432 | tf_op jit(solution)/shard_map/all_to_all | solution.py:45
  233.4 1.6 copy.48
  235.0 12.0 %all-to-all-done.2 = bf16[64,2,1536]{2,1,0:T(2,128)(2,1)S(1)} async-done(((bf16[64,2,1536]{2,1,0:T(2,128)(2,1)}), bf16[64,2,1536]{2,1,0:T(2,128)(2,1)S(1)}, u32[]{:S(2)}, u32[]{:S(2)}) %all-to-all-start.2) | async-done | bytes 393248 | tf_op jit(solution)/shard_map/all_to_all | solution.py:45
  247.5 8.7 %all_to_all.42 = bf16[2,64,3072]{2,1,0:T(8,128)(2,1)S(1)} all-to-all(bf16[2,64,3072]{2,1,0:T(8,128)(2,1)S(1)} %broadcast_in_dim.147), channel_id=1, replica_groups=mesh['ga_0'=8,'ga_1'=8,'ga_2'=2,'band'=4] {'ga_2'}, dimensions={0} | all-to-all | bytes 1572864 | tf_op jit(solution)/shard_map/all_to_all | solution.py:45
  256.2 1.7 copy.40
  257.9 4.0 convert_element_type.70
  262.0 2.7 fusion.9
  265.6 4.6 %all-to-all-start.5 = ((bf16[64,96,32]{1,2,0:T(8,128)(2,1)}), bf16[64,96,32]{1,2,0:T(8,128)(2,1)S(1)}, u32[]{:S(2)}, u32[]{:S(2)}) async-start(bf16[64,96,32]{1,2,0:T(8,128)(2,1)} %broadcast_in_dim.149), calls=%async_computation.5 | async-start | bytes 1048576 | tf_op jit(solution)/shard_map/all_to_all | solution.py:45
  270.3 17.9 %all-to-all-done.5 = bf16[64,96,32]{1,2,0:T(8,128)(2,1)S(1)} async-done(((bf16[64,96,32]{1,2,0:T(8,128)(2,1)}), bf16[64,96,32]{1,2,0:T(8,128)(2,1)S(1)}, u32[]{:S(2)}, u32[]{:S(2)}) %all-to-all-start.5) | async-done | bytes 393248 | tf_op jit(solution)/shard_map/all_to_all | solution.py:45
  288.3 5.8 %all_to_all.43 = bf16[2,64,96,32]{2,3,1,0:T(8,128)(2,1)S(1)} all-to-all(bf16[2,64,96,32]{2,3,1,0:T(8,128)(2,1)S(1)} %broadcast_in_dim.150), channel_id=1, replica_groups=mesh['ga_0'=8,'ga_1'=8,'ga_2'=2,'band'=4] {'ga_2'}, dimensions={0} | all-to-all | bytes 1572864 | tf_op jit(solution)/shard_map/all_to_all | solution.py:45
  294.1 3.1 copy.45
  297.1 110.9 %while.28 = (s32[]{:T(128)}, f32[256,32]{0,1:T(8,128)S(1)}, s32[12288]{0:T(1024)}, s32[1024]{0:T(1024)S(1)}, f32[256,12]{0,1:T(8,128)S(1)}, /*index=5*/f32[3,256...) while((s32[]{:T(128)}, f32[256,32]{0,1:T(8,128)S(1)}, ...), condition=%wide.region_5.8_spmd, body=%wide.region_4.7_spmd.sunk | while | flops 20952132 | bytes 4915043 | solution.py:208
  298.9 1.6 gather_fusion.2
  305.8 1.6 gather_fusion.2
  312.7 1.6 gather_fusion.2
  319.7 1.6 gather_fusion.2
  326.6 1.6 gather_fusion.2
  333.6 1.6 gather_fusion.2
  340.5 1.6 gather_fusion.2
  347.4 1.6 gather_fusion.2
  354.4 1.6 gather_fusion.2
  361.3 1.6 gather_fusion.2
  368.2 1.6 gather_fusion.2
  375.2 1.6 gather_fusion.2
  382.1 1.6 gather_fusion.2
  389.0 1.6 gather_fusion.2
  396.0 1.6 gather_fusion.2
  402.9 1.6 gather_fusion.2
  (948 shorter events, 173.9 us)
Async XLA Ops:
  0.0 1.7 copy-start
  7.2 2.9 copy-start.3
  15.7 3.0 copy-start.3
  24.1 3.0 copy-start.3
  32.6 3.0 copy-start.3
  41.0 3.0 copy-start.3
  49.5 3.0 copy-start.3
  57.9 3.0 copy-start.3
  66.3 3.0 copy-start.3
  74.8 3.0 copy-start.3
  83.2 3.0 copy-start.3
  91.7 3.0 copy-start.3
  100.1 3.0 copy-start.3
  108.6 3.0 copy-start.3
  117.0 3.0 copy-start.3
  125.5 3.0 copy-start.3
  133.9 3.0 copy-start.3
  137.1 4.1 copy-start.2
  158.7 33.9 %copy-start.5 = (bf16[96,3072]{1,0:T(8,128)(2,1)S(1)}, bf16[96,3072]{1,0:T(8,128)(2,1)}, u32[]{:S(2)}) copy-start(bf16[96,3072]{1,0:T(8,128)(2,1)} %param.16) | copy-start | bytes 1769476
  194.3 30.7 %all-to-all-start.4 = ((bf16[4,96,3072]{2,1,0:T(8,128)(2,1)}), bf16[4,96,3072]{2,1,0:T(8,128)(2,1)S(1)}, u32[]{:S(2)}, u32[]{:S(2)}) async-start(bf16[4,96,3072]{2,1,0:T(8,128)(2,1)} %broadcast_in_dim.148), calls=%async_computation.4 | async-start | bytes 4718592 | tf_op jit(solution)/shard_map/all_to_all | solution.py:45
  225.0 22.0 %all-to-all-start.2 = ((bf16[64,2,1536]{2,1,0:T(2,128)(2,1)}), bf16[64,2,1536]{2,1,0:T(2,128)(2,1)S(1)}, u32[]{:S(2)}, u32[]{:S(2)}) async-start(bf16[64,2,1536]{2,1,0:T(2,128)(2,1)} %reshape.1014), calls=%async_computation.2 | async-start | bytes 786432 | tf_op jit(solution)/shard_map/all_to_all | solution.py:45
  262.0 8.3 %copy-start.4 = (bf16[256,32]{0,1:T(8,128)(2,1)S(1)}, bf16[256,32]{0,1:T(8,128)(2,1)}, u32[]{:S(2)}) copy-start(bf16[256,32]{0,1:T(8,128)(2,1)} %get-tuple-element.716) | copy-start | bytes 49156
  265.6 22.6 %all-to-all-start.5 = ((bf16[64,96,32]{1,2,0:T(8,128)(2,1)}), bf16[64,96,32]{1,2,0:T(8,128)(2,1)S(1)}, u32[]{:S(2)}, u32[]{:S(2)}) async-start(bf16[64,96,32]{1,2,0:T(8,128)(2,1)} %broadcast_in_dim.149), calls=%async_computation.5 | async-start | bytes 1048576 | tf_op jit(solution)/shard_map/all_to_all | solution.py:45
  294.1 3.1 copy-start.1
where the time goes:
time: 413 us; the launch traced here: 409 us
  local copies, waits for them, and re-layouts  167 us (40%)
  blocking collectives  59.3 us (14%)
  waiting for transfers between devices  49.1 us (12%)
  other arithmetic  42.6 us (10%)
  loops' own time  38.2 us (9%)
  matrix products  35.5 us (9%)
  starting transfers between devices  17 us (4%)
    all_to_all x3, waiting for transfers between devices, from_everyone(): lax.all_to_all(jnp.broadcast_to(array[None], (devices, *array.shape)), ax...  49.1 us
    gather x32, local copies, waits for them, and re-layouts, beta_atoms(): place = jnp.take(positions, atoms, axis=1)  35.8 us
    another operation x1, loops' own time, shards(): lax.map(one_block, starts).reshape(NPROJ, nbands)  35.6 us
    gather x32, local copies, waits for them, and re-layouts, beta_atoms(): kind = jnp.take(species, atoms)  35.1 us
    all_to_all x1, blocking collectives, sum_by_axis(): lax.all_to_all(nearer, far, split_axis=0, concat_axis=0, tiled=True)  33.3 us
    dynamic_slice x32, local copies, waits for them, and re-layouts, beta_atoms(): lax.dynamic_slice_in_dim(proj_atom, jnp.asarray(start).astype(jnp.int32),...  24.9 us
    dot_general x16, matrix products, step(): return acc + jnp.dot(beta, rows, preferred_element_type=jnp.float32)  18.8 us
    all_to_all x3, starting transfers between devices, from_everyone(): lax.all_to_all(jnp.broadcast_to(array[None], (devices, *array.shape)), ax...  17 us
  transfers between devices with their start and end apart: 3, of which 3 were waited for; matrix products, arithmetic and copies ran while one was open for 2% of the time, Pallas kernels for 0%

commit v1 on v0

v1 whole, which is shorter than its diff:
```python
import math

import jax
import jax.numpy as jnp
from jax import lax
from jax.experimental import pallas as pl
from jax.experimental.pallas import tpu as pltpu
from jax.sharding import Mesh
from jax.sharding import PartitionSpec as P

NCH = 12
QBINS = 128
MMAX = 24
GA = ("z", "y", "core")
NZ, NY, NC, NX = 8, 8, 2, 4
PW = 256
BANDS = 32
ATOMS = 1024
LANE_ATOMS = 128
WIDTH = LANE_ATOMS * NCH
HALF = 6144
SCALE = 1.0 / math.sqrt(32768.0)
MESH = pl.DeviceIdType.MESH
FAR_FIRST = (4, 3, 5, 2, 6, 1, 7)
NEAR_FIRST = (1, 7, 2, 6, 3, 5, 4)
F32 = jnp.float32
BF16 = jnp.bfloat16


def dot(a, b, **kw):
    return jnp.dot(a, b, preferred_element_type=F32, **kw)


def split2(v):
    hi = v.astype(BF16)
    return hi, (v - hi.astype(F32)).astype(BF16)


def iota(shape, dim):
    return lax.broadcasted_iota(jnp.int32, shape, dim)


def horner(y, terms):
    acc = jnp.full_like(y, terms[-1])
    for term in terms[-2::-1]:
        acc = acc * y + term
    return acc


SIN_TERMS = [(-1) ** k * math.pi ** (2 * k + 1) / math.factorial(2 * k + 1) for k in range(6)]
COS_TERMS = [(-1) ** k * math.pi ** (2 * k) / math.factorial(2 * k) for k in range(6)]


def circle(turns):
    r = turns - jnp.floor(turns + 0.5)
    y = r * r
    s = r * horner(y, SIN_TERMS)
    c = horner(y, COS_TERMS)
    return 1.0 - 2.0 * s * s, 2.0 * s * c


def fold(v):
    v = v + pltpu.roll(v, 32, 1)
    return v + pltpu.roll(v, 64, 1)


def kernel(
    coeffs, miller, owner, species, positions, radial, coupling, out,
    cbuf, mtmp, beta, acc, place, rad_hi, rad_lo, sel_a, expand, own_f,
    rs_send, rs_recv, nbuf, wide, ball, xsend, xrecv, mx, fsend, frecv,
    a_s, a_r, rs_s, rs_r, g1_s, g1_r, g2_s, g2_r, b_s, b_r, b_l, x_s, x_r, e_s, e_r, f_s, f_r,
):
    z, y, c, x = (lax.axis_index(a) for a in ("z", "y", "core", "band"))
    barrier = pltpu.get_barrier_semaphore()

    def signal(to):
        pl.semaphore_signal(barrier, inc=1, device_id=to, device_id_type=MESH)

    for d in FAR_FIRST:
        signal((z, (y + d) % NY, c, x))
        for o in range(NC):
            signal(((z + d) % NZ, y, (c + o) % NC, x))
    for d in (2, 1, 3):
        for o in range(NC):
            signal((z, y, (c + o) % NC, (x + d) % NX))
    signal((z, y, 1 - c, x))
    greeted = 7 + 14 + 6 + 1

    def remote(src, dst, s, r, to):
        return pltpu.make_async_remote_copy(
            src_ref=src, dst_ref=dst, send_sem=s, recv_sem=r, device_id=to, device_id_type=MESH
        )

    mtmp[...] = jnp.zeros_like(mtmp)
    mtmp[0:3, :] = miller[...].astype(F32)
    cbuf[y, 0:32, :] = coeffs[...].astype(F32).T.astype(BF16)
    cbuf[y, 32:40, :] = mtmp[...].astype(BF16)

    col = iota((128, 128), 1)
    j, q, i = col >> 5, (col >> 1) & 15, col & 1
    first = NCH * ((((q >> 1) * NY + y) * NC + (q & 1)) * 8 + j * 2 + i)
    row_of, lane_of = first >> 7, first & 127
    ids = owner[...].astype(F32).T
    ids_hi = jnp.floor(ids * (1.0 / 32.0))
    ids_lo = ids - 32.0 * ids_hi
    pick = (iota((128, 128), 0) == row_of).astype(F32)[0:96, :].astype(BF16)
    at_row = 32.0 * dot(ids_hi.astype(BF16), pick) + dot(ids_lo.astype(BF16), pick)
    atom = jnp.sum(jnp.where(iota((128, 128), 0) == lane_of, at_row, 0.0), axis=0, keepdims=True)
    onehot = (iota((ATOMS, 128), 0) == atom.astype(jnp.int32)).astype(F32)
    place[...] = dot(positions[...], onehot, precision=lax.Precision.HIGHEST)
    kind = dot(species[...].astype(F32).astype(BF16), onehot.astype(BF16))

    atom_row = iota((128, WIDTH), 0)
    lane = iota((128, WIDTH), 1)
    off = lane - NCH * atom_row
    spread = ((off >= 0) & (off < NCH)).astype(F32).astype(BF16)
    kind_at = dot(kind.astype(BF16), spread)
    lane1 = iota((1, WIDTH), 1)
    chan = lane1 - NCH * jnp.floor((lane1.astype(F32) + 0.5) * (1.0 / NCH)).astype(jnp.int32)
    column = kind_at.astype(jnp.int32) * 3 + (chan >> 2)
    sel_a[...] = (
        ((atom_row & 15) == column) & (((atom_row >> 4) & 3) == (chan & 3))
    ).astype(F32).astype(BF16)

    krow = iota((256, WIDTH // 2), 0)
    klane = iota((256, WIDTH // 2), 1)
    koff = klane - NCH * (krow & 63)
    expand[...] = (
        (koff >= 0) & (koff < NCH) & (((koff & 3) == 0) == (krow < 128))
    ).astype(F32).astype(BF16)

    rsel = ((iota((128, 12), 0) & 15) == iota((128, 12), 1)).astype(F32)
    rad = dot(rsel, radial[...], precision=lax.Precision.HIGHEST).T
    hi, lo = split2(rad)
    rad_hi[...] = hi
    rad_lo[...] = lo
    acc[...] = jnp.zeros_like(acc)

    def part_y(yy):
        return cbuf.at[yy]

    def make_block(yy):
        m8 = mtmp[...]
        n2 = jnp.sum(m8 * m8, axis=0, keepdims=True)
        qv = n2 * ((QBINS - 1) / (3.0 * MMAX * MMAX))
        mt = jnp.where(iota((8, PW), 0) == 3, qv, m8).T
        lanes = iota((PW, 128), 1)
        m0, m1, m2, qcol = (
            jnp.broadcast_to(mt[:, k : k + 1], (PW, 128)) for k in range(4)
        )
        hats = jnp.maximum(0.0, 1.0 - jnp.abs(qcol - lanes.astype(F32)))
        h_hi, h_lo = split2(hats)
        radval = dot(h_hi, rad_hi[...]) + dot(h_lo, rad_hi[...]) + dot(h_hi, rad_lo[...])
        t = (lanes >> 4) & 3
        w = jnp.where(t == 1, m0, jnp.where(t == 2, m1, m2)) * (SCALE / MMAX)
        amp = radval * jnp.where(t == 0, SCALE, w)
        a_hi, a_lo = split2(amp)
        amp2 = jnp.where(lanes < 64, a_hi.astype(F32), a_lo.astype(F32)).astype(BF16)
        turns = m0 * place[0:1, :] + m1 * place[1:2, :] + m2 * place[2:3, :]
        cos, sin = circle(turns)
        parts = []
        for v in (cos, sin):
            vh = v.astype(BF16).astype(F32)
            vl = pltpu.roll(v - vh, 64, 1)
            parts.append((jnp.where(lanes < 64, vh, vl), jnp.where(lanes < 64, vl, vh)))
        for h in range(2):
            lhs = jnp.concatenate([parts[0][h], parts[1][h]], axis=1).astype(BF16)
            cols = slice(h * (WIDTH // 2), (h + 1) * (WIDTH // 2))
            phase = dot(lhs, expand[...])
            ampl = dot(amp2, sel_a[:, cols])
            block = (phase * ampl).astype(BF16)
            beta[yy, :, cols] = block
            acc[:, cols] += dot(cbuf[yy, 0:32, :], block)

    make_block(y)

    pl.semaphore_wait(barrier, greeted)
    a_out = []
    for d in FAR_FIRST:
        yy = (y + d) % NY
        cp = remote(part_y(y), part_y(y), a_s.at[d], a_r.at[y], (z, yy, c, x))
        cp.start()
        a_out.append(cp)

    side = x // 2
    slot = (x % 2) * NC + c
    home = ball.at[x % 2, pl.ds(96 * c, 96)]
    b_out = []
    for d in (2, 1, 3):
        cp = remote(coupling, home, b_s.at[d], b_r.at[slot], (z, y, side, (x + d) % NX))
        cp.start()
        b_out.append(cp)
    own_copy = pltpu.make_async_copy(coupling, home, b_l)
    partner_copy = remote(coupling, home, b_s.at[0], b_r.at[slot], (z, y, 1 - c, x))

    @pl.when(side == c)
    def _():
        own_copy.start()

    @pl.when(side != c)
    def _():
        partner_copy.start()

    def step(k, carry):
        d = jnp.where(k % 2 == 1, (k + 1) // 2, NY - k // 2)
        yy = (y + d) % NY
        remote(part_y(yy), part_y(yy), a_s.at[0], a_r.at[yy], (z, y, c, x)).wait_recv()
        mtmp[...] = cbuf[yy, 32:40, :].astype(F32)
        make_block(yy)
        return carry

    lax.fori_loop(1, NY, step, 0)

    stacked = jnp.concatenate([acc[:, 384 * k : 384 * (k + 1)] for k in range(4)], axis=0).T
    rs_send[...] = stacked.astype(BF16).reshape(16, 24, 128)
    sid = c * NZ + z
    rs_out = []
    for d in FAR_FIRST:
        for o in range(NC):
            zz, cc = (z + d) % NZ, (c + o) % NC
            cp = remote(rs_send.at[cc * NZ + zz], rs_recv.at[sid], rs_s.at[d * 2 + o], rs_r.at[sid], (zz, y, cc, x))
            cp.start()
            rs_out.append(cp)
    cp = remote(rs_send.at[(1 - c) * NZ + z], rs_recv.at[sid], rs_s.at[1], rs_r.at[sid], (z, y, 1 - c, x))
    cp.start()
    rs_out.append(cp)

    def wait16(buf, sems, s):
        remote(buf.at[s], buf.at[s], rs_s.at[0], sems.at[s], (z, y, c, x)).wait_recv()

    total = rs_send[sid].astype(F32)
    order16 = [(0, 1)] + [(d, o) for d in NEAR_FIRST for o in range(NC)]
    for d, o in order16:
        s = ((c + o) % NC) * NZ + (z + d) % NZ
        wait16(rs_recv, rs_r, s)
        total = total + rs_recv[s].astype(F32)

    fm = z + c * (y - z)
    sm = y + c * (z - y)

    def at_first(f):
        return (z + (1 - c) * (f - z), y + c * (f - y), c, x)

    def at_second(s):
        return (z + c * (s - z), y + (1 - c) * (s - y), c, x)

    nbuf[sm, fm] = total.astype(BF16)
    g_out = []
    for d in FAR_FIRST:
        ff = (fm + d) % 8
        cp = remote(nbuf.at[sm, fm], nbuf.at[sm, fm], g1_s.at[d], g1_r.at[fm], at_first(ff))
        cp.start()
        g_out.append(cp)
    for d in NEAR_FIRST:
        ff = (fm + d) % 8
        remote(nbuf.at[sm, ff], nbuf.at[sm, ff], g1_s.at[0], g1_r.at[ff], (z, y, c, x)).wait_recv()
    for d in FAR_FIRST:
        ss = (sm + d) % 8
        cp = remote(nbuf.at[sm], nbuf.at[sm], g2_s.at[d], g2_r.at[sm], at_second(ss))
        cp.start()
        g_out.append(cp)

    group = iota((24, 128), 1) >> 5

    def spread_row(s):
        def one(f, carry):
            zz = f + c * (s - f)
            yy = s + c * (f - s)
            n = (zz // 2) * 16 + yy * 2 + zz % 2
            piece = nbuf[s, f].astype(F32)
            for k in range(4):
                wide[n, 24 * k : 24 * (k + 1), :] = jnp.where(group == k, piece, 0.0).astype(BF16)
            return carry

        lax.fori_loop(0, 8, one, 0)

    spread_row(sm)
    for d in NEAR_FIRST:
        ss = (sm + d) % 8
        remote(nbuf.at[ss], nbuf.at[ss], g1_s.at[0], g2_r.at[ss], (z, y, c, x)).wait_recv()
        spread_row(ss)

    for xh in range(2):
        for cs in range(2):
            here = ball.at[xh, pl.ds(96 * cs, 96)]
            mine = (2 * c + xh == x) & (c == cs)

            @pl.when(mine)
            def _():
                own_copy.wait()

            @pl.when(jnp.logical_not(mine))
            def _():
                remote(coupling, here, b_s.at[0], b_r.at[xh * NC + cs], (z, y, c, x)).wait_recv()

    part = jnp.zeros((192, 128), F32)
    for xh in range(2):
        part = part + dot(ball[xh], wide[32 * xh : 32 * (xh + 1)].reshape(3072, 128))
    part = fold(part)
    packs = []
    for r in range(2):
        pack = jnp.zeros((24, 128), F32)
        for k in range(4):
            pack = jnp.where(group == k, part[96 * r + 24 * k : 96 * r + 24 * (k + 1)], pack)
        packs.append(pack)
    xsend[...] = jnp.where(c == 0, packs[1], packs[0])
    xcp = remote(xsend, xrecv, x_s, x_r, (z, y, 1 - c, x))
    xcp.start()
    own = jnp.where(c == 0, packs[0], packs[1])
    xcp.wait()
    qm = 2 * z + c
    mx[qm] = (own + xrecv[...]).astype(BF16)

    e_out = []
    for d in FAR_FIRST:
        for o in range(NC):
            zz, cc = (z + d) % NZ, (c + o) % NC
            cp = remote(mx.at[qm], mx.at[qm], e_s.at[d * 2 + o], e_r.at[qm], (zz, y, cc, x))
            cp.start()
            e_out.append(cp)
    cp = remote(mx.at[qm], mx.at[qm], e_s.at[1], e_r.at[qm], (z, y, 1 - c, x))
    cp.start()
    e_out.append(cp)
    for d, o in order16:
        wait16(mx, e_r, 2 * ((z + d) % NZ) + (c + o) % NC)

    mv = mx[...].astype(F32).reshape(384, 128)
    g384 = iota((384, 128), 1) >> 5
    rhs = jnp.concatenate([jnp.where(g384 == k, mv, 0.0) for k in range(4)], axis=0).astype(BF16)
    g64 = iota((64, 128), 1) >> 5

    def partial(yy):
        full = fold(dot(beta[yy], rhs))
        pack = full[0:64]
        for k in range(1, 4):
            pack = jnp.where(g64 == k, full[64 * k : 64 * (k + 1)], pack)
        return pack

    f_out = []
    for d in FAR_FIRST:
        yy = (y + d) % NY
        fsend[yy] = partial(yy).astype(BF16)
        cp = remote(fsend.at[yy], frecv.at[y], f_s.at[d], f_r.at[y], (z, yy, c, x))
        cp.start()
        f_out.append(cp)
    total = partial(y)
    for d in NEAR_FIRST:
        yy = (y + d) % NY
        remote(frecv.at[yy], frecv.at[yy], f_s.at[0], f_r.at[yy], (z, y, c, x)).wait_recv()
        total = total + frecv[yy].astype(F32)
    for k in range(4):
        out[64 * k : 64 * (k + 1), :] = total[:, 32 * k : 32 * (k + 1)]

    for cp in a_out + b_out + rs_out + g_out + e_out + f_out:
        cp.wait_send()

    @pl.when(side != c)
    def _():
        partner_copy.wait_send()


def shards(coeffs, coupling, miller, species, proj_atom, positions, radial):
    vmem = pl.BlockSpec(memory_space=pltpu.VMEM)
    dma = pltpu.SemaphoreType.DMA
    change = pl.pallas_call(
        kernel,
        out_shape=jax.ShapeDtypeStruct((PW, BANDS), F32),
        in_specs=[vmem] * 6 + [pl.BlockSpec(memory_space=pl.ANY)],
        out_specs=vmem,
        scratch_shapes=[
            pltpu.VMEM((NY, 40, PW), BF16),
            pltpu.VMEM((8, PW), F32),
            pltpu.VMEM((NY, PW, WIDTH), BF16),
            pltpu.VMEM((BANDS, WIDTH), F32),
            pltpu.VMEM((3, 128), F32),
            pltpu.VMEM((128, 128), BF16),
            pltpu.VMEM((128, 128), BF16),
            pltpu.VMEM((128, WIDTH), BF16),
            pltpu.VMEM((256, WIDTH // 2), BF16),
            pltpu.VMEM((8, 128), F32),
            pltpu.VMEM((16, 24, 128), BF16),
            pltpu.VMEM((16, 24, 128), BF16),
            pltpu.VMEM((8, 8, 24, 128), BF16),
            pltpu.VMEM((64, 96, 128), BF16),
            pltpu.VMEM((2, 192, 3072), BF16),
            pltpu.VMEM((24, 128), F32),
            pltpu.VMEM((24, 128), F32),
            pltpu.VMEM((16, 24, 128), BF16),
            pltpu.VMEM((NY, 64, 128), BF16),
            pltpu.VMEM((NY, 64, 128), BF16),
            dma((8,)), dma((8,)), dma((16,)), dma((16,)), dma((8,)), dma((8,)), dma((8,)), dma((8,)),
            dma((4,)), dma((4,)), dma, dma, dma, dma((16,)), dma((16,)), dma((8,)), dma((8,)),
        ],
        compiler_params=pltpu.CompilerParams(
            collective_id=0, has_side_effects=True, vmem_limit_bytes=48 * 1024 * 1024
        ),
    )(
        coeffs, miller, proj_atom.reshape(96, 128), species.reshape(1, ATOMS), positions, radial, coupling
    )
    return (coeffs.astype(F32) + change).astype(BF16)


def solution(mesh):
    torus = Mesh(mesh.devices.reshape(NZ, NY, NC, NX), ("z", "y", "core", "band"))
    return jax.shard_map(
        shards,
        mesh=torus,
        in_specs=(P(GA, "band"), P(GA, "band"), P(None, GA), P(), P(), P(), P()),
        out_specs=P(GA, "band"),
        check_vma=False,
    )
```

time: 413 us -> 65.1 us (0.16)
  local copies, waits for them, and re-layouts: 167 us -> 2.77 us
  Pallas kernels: 0 us -> 62 us
  blocking collectives: 59.3 us -> 0 us
  waiting for transfers between devices: 49.1 us -> 0 us
  other arithmetic: 42.6 us -> 0.02 us
  loops' own time: 38.2 us -> 0 us
  matrix products: 35.5 us -> 0 us
  starting transfers between devices: 17 us -> 0 us
    gather x64 -> x0, local copies, waits for them, and re-layouts: 70.9 us -> none  [the longest x32 35.8 us: beta_atoms(): place = jnp.take(positions, atoms, axis=1)]
    pallas_call x0 -> x1, Pallas kernels: none -> 62 us  [shards(): pl.pallas_call(kernel, out_shape=jax.ShapeDtypeStruct((PW, BANDS), F32),...]
    all_to_all x4 -> x0, blocking collectives: 59.3 us -> none  [the longest x1 33.3 us: sum_by_axis(): lax.all_to_all(nearer, far, split_axis=0, concat_axis=0, tiled=True)]
    all_to_all x3 -> x0, waiting for transfers between devices: 49.1 us -> none  [from_everyone(): lax.all_to_all(jnp.broadcast_to(array[None], (devices, *array.shape)), ax...]
    another operation x2 -> x0, loops' own time: 38.2 us -> none  [the longest x1 35.6 us: shards(): lax.map(one_block, starts).reshape(NPROJ, nbands)]
    dynamic_slice x48 -> x0, local copies, waits for them, and re-layouts: 35.8 us -> none  [the longest x32 24.9 us: beta_atoms(): lax.dynamic_slice_in_dim(proj_atom, jnp.asarray(start).astype(jnp.int32),...]
    dot_general x66 -> x0, matrix products: 35.5 us -> none  [the longest x16 18.8 us: step(): return acc + jnp.dot(beta, rows, preferred_element_type=jnp.float32)]
    all_to_all x3 -> x0, starting transfers between devices: 17 us -> none  [from_everyone(): lax.all_to_all(jnp.broadcast_to(array[None], (devices, *array.shape)), ax...]
  transfers between devices with their start and end apart: 3 -> 0, of which waited for: 3 -> 0; matrix products, arithmetic and copies ran while one was open for 2% -> 0% of each run, Pallas kernels for 0% -> 0%
where the time goes in v1:
time: 65.1 us; the launch traced here: 64.9 us
  Pallas kernels  62 us (95%)
  local copies, waits for them, and re-layouts  2.77 us (4%)
    pallas_call x1, Pallas kernels, shards(): pl.pallas_call(kernel, out_shape=jax.ShapeDtypeStruct((PW, BANDS), F32),...  62 us
    unnamed x15, local copies, waits for them, and re-layouts  1.97 us

profile of v1, /device:TPU:1, one launch (start us, length us, event | category | flops | bytes accessed | tf_op | source)
XLA Modules:
  0.0 64.9 jit_solution(15851644525111318344)
XLA Ops:
  0.0 0.0 copy-start.1
  0.0 0.0 copy-start.2
  0.0 0.0 copy-start.3
  0.0 0.0 copy-start.4
  0.0 0.0 copy-start.5
  0.0 0.9 %copy.11.coeffs = bf16[256,32]{1,0:T(8,128)(2,1)S(1)} copy(bf16[256,32]{0,1:T(8,128)(2,1)} %param.7) | data formatting | bytes 32768 | tf_op args[0]
  0.9 0.0 copy-done.1
  0.9 0.0 copy-done.2
  0.9 0.0 copy-done.3
  0.9 0.0 copy-done.4
  1.0 0.0 copy-done.5
  1.0 0.0 copy-start
  1.0 1.1 %copy-done = bf16[96,3072]{1,0:T(8,128)(2,1)S(1)} copy-done((bf16[96,3072]{1,0:T(8,128)(2,1)S(1)}, bf16[96,3072]{1,0:T(8,128)(2,1)}, u32[]{:S(2)}) %copy-start) | copy-done | bytes 589848
  2.0 0.0 copy-start.6
  2.0 62.0 %shard_map.73 = f32[256,32]{1,0:T(8,128)S(1)} custom-call(bf16[256,32]{1,0:T(8,128)(2,1)S(1)} %copy.11.coeffs, s32[3,256]{1,0:T(4,128)S(1)} %copy-done.4, s32[96,128]{1,0:T(8,128)S(1)} %bitcast.2, s32[1,1024]{1,0:T(1,128)S(1)} %bitcast.3, f32[3,1024]{1,0:T(4,128)S(1)} %copy-done.2, f32[12,128]{1,0:T(8,128)S(1)} %copy-done.3, bf16[96,3072]{1,0:T(8,128)(2,1)S(1)} %copy-done), custom_call_target="tpu_custom_call" | custom-call | tf_op jit(solution)/shard_map/pallas_call | solution.py:365
  64.0 0.0 copy-done.6
  64.0 0.1 copy.12
  64.2 0.7 %copy.13 = bf16[256,32]{0,1:T(8,128)(2,1)} copy(bf16[256,32]{1,0:T(8,128)(2,1)S(1)} %add_convert_fusion) | data formatting | bytes 32768 | tf_op jit(solution)/shard_map/convert_element_type | solution.py:400
  (1 shorter events, 0.0 us)
Async XLA Ops:
  0.0 0.9 %copy-start.1 = (s32[12288]{0:T(1024)S(1)}, s32[12288]{0:T(1024)}, u32[]{:S(2)}) copy-start(s32[12288]{0:T(1024)} %param.11) | copy-start | bytes 147460
  0.0 0.9 %copy-start.2 = (f32[3,1024]{1,0:T(4,128)S(1)}, f32[3,1024]{1,0:T(4,128)}, u32[]{:S(2)}) copy-start(f32[3,1024]{1,0:T(4,128)} %positions.1) | copy-start | bytes 36868
  0.0 0.9 %copy-start.3 = (f32[12,128]{1,0:T(8,128)S(1)}, f32[12,128]{1,0:T(8,128)}, u32[]{:S(2)}) copy-start(f32[12,128]{1,0:T(8,128)} %radial.1) | copy-start | bytes 18436
  0.0 0.9 %copy-start.4 = (s32[3,256]{1,0:T(4,128)S(1)}, s32[3,256]{1,0:T(4,128)}, u32[]{:S(2)}) copy-start(s32[3,256]{1,0:T(4,128)} %miller.1) | copy-start | bytes 9220
  0.0 0.9 %copy-start.5 = (s32[1024]{0:T(1024)S(1)}, s32[1024]{0:T(1024)}, u32[]{:S(2)}) copy-start(s32[1024]{0:T(1024)} %param.10) | copy-start | bytes 12292
  1.0 1.1 %copy-start = (bf16[96,3072]{1,0:T(8,128)(2,1)S(1)}, bf16[96,3072]{1,0:T(8,128)(2,1)}, u32[]{:S(2)}) copy-start(bf16[96,3072]{1,0:T(8,128)(2,1)} %coupling.1) | copy-start | bytes 1769476
  2.0 62.0 %copy-start.6 = (bf16[256,32]{0,1:T(8,128)(2,1)S(1)}, bf16[256,32]{0,1:T(8,128)(2,1)}, u32[]{:S(2)}) copy-start(bf16[256,32]{0,1:T(8,128)(2,1)} %param.7) | copy-start | bytes 49156

commit v2 on v1

v2 whole, which is shorter than its diff:
```python
import math

import jax
import jax.numpy as jnp
from jax import lax
from jax.experimental import pallas as pl
from jax.experimental.pallas import tpu as pltpu
from jax.sharding import Mesh
from jax.sharding import PartitionSpec as P

NCH = 12
QBINS = 128
MMAX = 24
GA = ("z", "y", "core")
NZ, NY, NC, NX = 8, 8, 2, 4
PW = 256
BANDS = 32
ATOMS = 1024
LANE_ATOMS = 128
ROWS = 64
WIDTH = LANE_ATOMS * NCH
HALF = 6144
SCALE = 1.0 / math.sqrt(32768.0)
MESH = pl.DeviceIdType.MESH
FAR_FIRST = (4, 5, 3, 6, 2, 7, 1)
NEAR_FIRST = (1, 7, 2, 6, 3, 5, 4)
PLACE = {0: 0, 1: 1, 7: 2, 2: 3, 6: 4, 3: 5, 5: 6, 4: 7}
BATCHES = ((0, 5), (5, 8))
F32 = jnp.float32
BF16 = jnp.bfloat16


def dot(a, b, **kw):
    return jnp.dot(a, b, preferred_element_type=F32, **kw)


def split2(v):
    hi = v.astype(BF16)
    return hi, (v - hi.astype(F32)).astype(BF16)


def iota(shape, dim):
    return lax.broadcasted_iota(jnp.int32, shape, dim)


def horner(y, terms):
    acc = jnp.full_like(y, terms[-1])
    for term in terms[-2::-1]:
        acc = acc * y + term
    return acc


SIN_TERMS = (
    3.141592640130705,
    -5.1677100835078935,
    2.5500775232145623,
    -0.5982912856196194,
    0.07765766030331765,
)
COS_TERMS = (
    0.9999999997799042,
    -4.934802137078829,
    4.058709159556242,
    -1.3352120030494103,
    0.2349373138103021,
    -0.024396324339225423,
)


def circle(turns):
    r = turns - jnp.floor(turns + 0.5)
    y = r * r
    s = r * horner(y, SIN_TERMS)
    c = horner(y, COS_TERMS)
    return 1.0 - 2.0 * s * s, 2.0 * s * c


def fold(v):
    v = v + pltpu.roll(v, 32, 1)
    return v + pltpu.roll(v, 64, 1)


def kernel(
    coeffs_h, miller_h, owner_h, species_h, positions_h, radial_h, coupling, out,
    miller, owner, species, positions, radial, in_s, cbuf, mtmp, beta, acc, place, rad3, rad_top, rad_low, perm, back,
    rs_send, rs_recv, nbuf, wide, ball, xsend, xrecv, mx, fsend, frecv,
    a_s, a_r, rs_s, rs_r, g1_s, g1_r, g2_s, g2_r, b_s, b_r, b_l, x_s, x_r, e_s, e_r, f_s, f_r,
):
    z, y, c, x = (lax.axis_index(a) for a in ("z", "y", "core", "band"))
    barrier = pltpu.get_barrier_semaphore()

    loads = [
        pltpu.make_async_copy(src, dst, in_s.at[k])
        for k, (src, dst) in enumerate(
            (
                (miller_h, miller), (coeffs_h, cbuf.at[y, 0:32]), (owner_h, owner),
                (radial_h, radial), (positions_h, positions), (species_h, species),
            )
        )
    ]
    for cp in loads[:2]:
        cp.start()

    def signal(to):
        pl.semaphore_signal(barrier, inc=1, device_id=to, device_id_type=MESH)

    for d in FAR_FIRST:
        signal((z, (y + d) % NY, c, x))
        for o in range(NC):
            signal(((z + d) % NZ, y, (c + o) % NC, x))
    for d in (2, 1, 3):
        for o in range(NC):
            signal((z, y, (c + o) % NC, (x + d) % NX))
    signal((z, y, 1 - c, x))
    greeted = 7 + 14 + 6 + 1

    def remote(src, dst, s, r, to):
        return pltpu.make_async_remote_copy(
            src_ref=src, dst_ref=dst, send_sem=s, recv_sem=r, device_id=to, device_id_type=MESH
        )
    for cp in loads[2:]:
        cp.start()
    for cp in loads[:2]:
        cp.wait()

    mtmp[...] = jnp.zeros_like(mtmp)
    mtmp[0:3, :] = miller[...].astype(F32)
    cbuf[y, 32:40, :] = mtmp[...].astype(BF16)

    pl.semaphore_wait(barrier, greeted)

    a_out = []
    for d in NEAR_FIRST:
        yy = (y + d) % NY
        cp = remote(cbuf.at[y], cbuf.at[y], a_s.at[d], a_r.at[y], (z, yy, c, x))
        cp.start()
        a_out.append(cp)

    side = x // 2

    def half_of(xs, cs, h):
        return ball.at[xs % 2, pl.ds(96 * cs + 48 * h, 48)], 4 * (xs % 2) + 2 * cs + h

    b_out, own_copies, partner_copies = [], [], []
    for first in range(2):
        for way, dx in enumerate((1, 3)):
            h = first if way == 0 else 1 - first
            spot, sem = half_of(x, c, h)
            cp = remote(
                coupling.at[48 * h : 48 * (h + 1)], spot, b_s.at[2 * way + h], b_r.at[sem], (z, y, side, (x + dx) % NX)
            )
            cp.start()
            b_out.append(cp)
    for h in range(2):
        spot, sem = half_of(x, c, h)
        rows = coupling.at[48 * h : 48 * (h + 1)]
        own_copies.append(pltpu.make_async_copy(rows, spot, b_l.at[h]))
        partner_copies.append(remote(rows, spot, b_s.at[4 + h], b_r.at[sem], (z, y, 1 - c, x)))

    @pl.when(side == c)
    def _():
        for cp in own_copies:
            cp.start()

    @pl.when(side != c)
    def _():
        for cp in partner_copies:
            cp.start()

    def moved(natural, ours):
        atom_of = jnp.floor((natural.astype(F32) + 0.5) * (1.0 / NCH)).astype(jnp.int32)
        return (ours == (natural - NCH * atom_of) * 32 + atom_of).astype(F32).astype(BF16)

    square = (384, 384)
    perm[...] = moved(iota(square, 0), iota(square, 1))
    back[...] = moved(iota(square, 1), iota(square, 0))
    acc[...] = jnp.zeros_like(acc)

    for cp in loads[2:]:
        cp.wait()
    col = iota((128, 128), 1)
    j, q, i = col >> 5, (col >> 1) & 15, col & 1
    first = NCH * ((((q >> 1) * NY + y) * NC + (q & 1)) * 8 + j * 2 + i)
    row_of, lane_of = first >> 7, first & 127
    ids = owner[...].astype(F32).T
    ids_hi = jnp.floor(ids * (1.0 / 32.0))
    ids_lo = ids - 32.0 * ids_hi
    pick = (iota((128, 128), 0) == row_of).astype(F32)[0:96, :].astype(BF16)
    at_row = 32.0 * dot(ids_hi.astype(BF16), pick) + dot(ids_lo.astype(BF16), pick)
    atom = jnp.sum(jnp.where(iota((128, 128), 0) == lane_of, at_row, 0.0), axis=0, keepdims=True)
    onehot = (iota((ATOMS, 128), 0) == atom.astype(jnp.int32)).astype(F32)
    place[...] = dot(positions[...], onehot, precision=lax.Precision.HIGHEST)
    kind = dot(species[...].astype(F32).astype(BF16), onehot.astype(BF16))

    rsel = ((iota((128, 12), 0) & 15) == iota((128, 12), 1)).astype(F32)
    rad = dot(rsel, radial[...], precision=lax.Precision.HIGHEST).T * SCALE
    kind3 = 3 * kind.astype(jnp.int32)
    row = iota((128, 128), 0)
    pick_s = jnp.concatenate([(row == kind3 + k).astype(F32) for k in range(3)], axis=1)
    hi, lo = split2(dot(rad, pick_s, precision=lax.Precision.HIGHEST))
    rad_top[0:128, :] = hi
    rad_top[128:256, :] = hi
    rad_low[...] = lo

    def make_block(yy, slot):
        m8 = cbuf[yy, 32:40, :].astype(F32)
        n2 = jnp.sum(m8 * m8, axis=0, keepdims=True)
        qv = n2 * ((QBINS - 1) / (3.0 * MMAX * MMAX))
        mt = jnp.where(iota((8, PW), 0) == 3, qv, m8).T
        hats = jnp.maximum(0.0, 1.0 - jnp.abs(mt[:, 3:4] - iota((PW, 128), 1).astype(F32)))
        h_hi, h_lo = split2(hats)
        rad3[...] = dot(jnp.concatenate([h_hi, h_lo], axis=1), rad_top[...]) + dot(h_hi, rad_low[...])
        for rows in (slice(r, r + ROWS) for r in range(0, PW, ROWS)):
            m0, m1, m2 = (jnp.broadcast_to(mt[rows, k : k + 1], (ROWS, 128)) for k in range(3))
            turns = m0 * place[0:1, :] + m1 * place[1:2, :] + m2 * place[2:3, :]
            cos, sin = circle(turns)
            sin = sin * (1.0 / MMAX)
            phases = (cos, m0 * sin, m1 * sin, m2 * sin)
            for k in range(3):
                amp = rad3[rows, 128 * k : 128 * (k + 1)]
                for t in range(4):
                    ch = 4 * k + t
                    beta[slot, rows, 128 * ch : 128 * (ch + 1)] = (amp * phases[t]).astype(BF16)
        acc[...] += dot(cbuf[yy, 0:32, :], beta[slot])

    make_block(y, 7)

    def step(k, carry):
        d = jnp.where(k % 2 == 1, (k + 1) // 2, NY - k // 2)
        yy = (y + d) % NY
        remote(cbuf.at[yy], cbuf.at[yy], a_s.at[0], a_r.at[yy], (z, y, c, x)).wait_recv()
        make_block(yy, 7 - k)
        return carry

    lax.fori_loop(1, NY, step, 0)

    g32 = iota((32, 128), 1) >> 5

    def lane_tile(j, g):
        tile = jnp.zeros((32, 128), F32)
        for k in range(4):
            chan = acc[:, 128 * (4 * g + k) : 128 * (4 * g + k + 1)]
            if k != j:
                chan = pltpu.roll(chan, (32 * (k - j)) % 128, 1)
            tile = jnp.where(g32 == k, chan, tile)
        return tile

    stacked = jnp.concatenate(
        [jnp.concatenate([lane_tile(j, g) for g in range(3)], axis=1) for j in range(4)], axis=0
    ).T.astype(BF16)
    rs_send[...] = dot(perm[...], stacked).astype(BF16).reshape(16, 24, 128)
    sid = c * NZ + z
    rs_out = []
    for d in FAR_FIRST:
        for o in range(NC):
            zz, cc = (z + d) % NZ, (c + o) % NC
            cp = remote(rs_send.at[cc * NZ + zz], rs_recv.at[sid], rs_s.at[d * 2 + o], rs_r.at[sid], (zz, y, cc, x))
            cp.start()
            rs_out.append(cp)
    cp = remote(rs_send.at[(1 - c) * NZ + z], rs_recv.at[sid], rs_s.at[1], rs_r.at[sid], (z, y, 1 - c, x))
    cp.start()
    rs_out.append(cp)

    near = 2 * c + 1 - x % 2
    which = jnp.where((near + 1) % NX == x, 0, 1)
    for cs in range(2):
        spot, sem = half_of(near, cs, which)
        remote(spot, spot, b_s.at[0], b_r.at[sem], (z, y, c, x)).wait_recv()
        cp = remote(spot, spot, b_s.at[6 + cs], b_r.at[sem], (z, y, c, (near + 2) % NX))
        cp.start()
        b_out.append(cp)

    def wait16(buf, sems, s):
        remote(buf.at[s], buf.at[s], rs_s.at[0], sems.at[s], (z, y, c, x)).wait_recv()

    total = rs_send[sid].astype(F32)
    order16 = [(0, 1)] + [(d, o) for d in NEAR_FIRST for o in range(NC)]
    for d, o in order16:
        s = ((c + o) % NC) * NZ + (z + d) % NZ
        wait16(rs_recv, rs_r, s)
        total = total + rs_recv[s].astype(F32)

    fm = z + c * (y - z)
    sm = y + c * (z - y)

    def at_first(f):
        return (z + (1 - c) * (f - z), y + c * (f - y), c, x)

    def at_second(s):
        return (z + c * (s - z), y + (1 - c) * (s - y), c, x)

    nbuf[sm, 0] = total.astype(BF16)
    g_out = []
    for d in FAR_FIRST:
        k = PLACE[(8 - d) % 8]
        cp = remote(nbuf.at[sm, 0], nbuf.at[sm, k], g1_s.at[d], g1_r.at[k], at_first((fm + d) % 8))
        cp.start()
        g_out.append(cp)
    for batch, (low, high) in enumerate(BATCHES):
        for k in range(max(low, 1), high):
            remote(nbuf.at[sm, k], nbuf.at[sm, k], g1_s.at[0], g1_r.at[k], (z, y, c, x)).wait_recv()
        rows = nbuf.at[sm, low:high]
        for d in FAR_FIRST:
            cp = remote(rows, rows, g2_s.at[batch, d], g2_r.at[batch, sm], at_second((sm + d) % 8))
            cp.start()
            g_out.append(cp)

    group = iota((24, 128), 1) >> 5

    masks = [(group == j).astype(F32).astype(BF16) for j in range(4)]

    def spread_rows(s, low, high):
        for k in range(low, high):
            f = (fm + ((k + 1) // 2 if k % 2 else 8 - k // 2)) % 8
            zz = f + c * (s - f)
            yy = s + c * (f - s)
            n = (zz // 2) * 16 + yy * 2 + zz % 2
            piece = nbuf[s, k]
            for j in range(4):
                wide[n, 24 * j : 24 * (j + 1), :] = piece * masks[j]

    spread_rows(sm, 0, 8)
    for batch, (low, high) in enumerate(BATCHES):
        for d in NEAR_FIRST:
            ss = (sm + d) % 8
            rows = nbuf.at[ss, low:high]
            remote(rows, rows, g1_s.at[0], g2_r.at[batch, ss], (z, y, c, x)).wait_recv()
            spread_rows(ss, low, high)

    for xh in range(2):
        for cs in range(2):
            for h in range(2):
                xs = 2 * c + xh
                mine = (xs == x) & (c == cs)
                passed = (xs == near) & (which == h)
                spot, sem = half_of(xs, cs, h)

                @pl.when(mine)
                def _():
                    own_copies[h].wait()

                @pl.when(jnp.logical_not(mine | passed))
                def _():
                    remote(spot, spot, b_s.at[0], b_r.at[sem], (z, y, c, x)).wait_recv()

    part = jnp.zeros((192, 128), F32)
    for xh in range(2):
        part = part + dot(ball[xh], wide[32 * xh : 32 * (xh + 1)].reshape(3072, 128))
    part = fold(part)
    packs = []
    for r in range(2):
        pack = jnp.zeros((24, 128), F32)
        for k in range(4):
            pack = jnp.where(group == k, part[96 * r + 24 * k : 96 * r + 24 * (k + 1)], pack)
        packs.append(pack)
    xsend[...] = jnp.where(c == 0, packs[1], packs[0])
    xcp = remote(xsend, xrecv, x_s, x_r, (z, y, 1 - c, x))
    xcp.start()
    own = jnp.where(c == 0, packs[0], packs[1])
    xcp.wait()
    qm = 2 * z + c
    mx[qm] = (own + xrecv[...]).astype(BF16)

    e_out = []
    for d in FAR_FIRST:
        for o in range(NC):
            zz, cc = (z + d) % NZ, (c + o) % NC
            cp = remote(mx.at[qm], mx.at[qm], e_s.at[d * 2 + o], e_r.at[qm], (zz, y, cc, x))
            cp.start()
            e_out.append(cp)
    cp = remote(mx.at[qm], mx.at[qm], e_s.at[1], e_r.at[qm], (z, y, 1 - c, x))
    cp.start()
    e_out.append(cp)
    for d, o in order16:
        wait16(mx, e_r, 2 * ((z + d) % NZ) + (c + o) % NC)

    ours = dot(back[...], mx[...].reshape(384, 128))
    ours = ours.T

    def channel(k):
        tile = jnp.zeros((32, 128), F32)
        for j in range(4):
            part = ours[32 * j : 32 * (j + 1), 128 * (k // 4) : 128 * (k // 4 + 1)]
            if k % 4 != j:
                part = pltpu.roll(part, (32 * (j - k % 4)) % 128, 1)
            tile = jnp.where(g32 == j, part, tile)
        return tile

    lhs = jnp.concatenate([channel(k) for k in range(NCH)], axis=1).astype(BF16)

    f_out = []
    for pair in range(4):
        both = lax.dot_general(
            lhs, beta[2 * pair : 2 * pair + 2].reshape(2 * PW, WIDTH),
            (((1,), (1,)), ((), ())), preferred_element_type=F32,
        )
        for half in range(2):
            total = both[:, PW * half : PW * (half + 1)]
            slot = 2 * pair + half
            if slot == 7:
                break
            d = FAR_FIRST[slot]
            yy = (y + d) % NY
            fsend[slot] = total.astype(BF16)
            cp = remote(fsend.at[slot], frecv.at[y], f_s.at[d], f_r.at[y], (z, yy, c, x))
            cp.start()
            f_out.append(cp)
    for d in NEAR_FIRST:
        yy = (y + d) % NY
        remote(frecv.at[yy], frecv.at[yy], f_s.at[0], f_r.at[yy], (z, y, c, x)).wait_recv()
        total = total + frecv[yy].astype(F32)
    out[...] = total

    for cp in a_out + b_out + rs_out + g_out + e_out + f_out:
        cp.wait_send()

    @pl.when(side != c)
    def _():
        for cp in partner_copies:
            cp.wait_send()


def shards(coeffs, coupling, miller, species, proj_atom, positions, radial):
    vmem = pl.BlockSpec(memory_space=pltpu.VMEM)
    dma = pltpu.SemaphoreType.DMA
    change = pl.pallas_call(
        kernel,
        out_shape=jax.ShapeDtypeStruct((BANDS, PW), F32),
        in_specs=[pl.BlockSpec(memory_space=pl.ANY)] * 7,
        out_specs=vmem,
        scratch_shapes=[
            pltpu.VMEM((3, PW), jnp.int32),
            pltpu.VMEM((96, 128), jnp.int32),
            pltpu.VMEM((1, ATOMS), jnp.int32),
            pltpu.VMEM((3, ATOMS), F32),
            pltpu.VMEM((12, QBINS), F32),
            dma((6,)),
            pltpu.VMEM((NY, 40, PW), BF16),
            pltpu.VMEM((8, PW), F32),
            pltpu.VMEM((NY, PW, WIDTH), BF16),
            pltpu.VMEM((BANDS, WIDTH), F32),
            pltpu.VMEM((3, 128), F32),
            pltpu.VMEM((PW, 384), F32),
            pltpu.VMEM((256, 384), BF16),
            pltpu.VMEM((128, 384), BF16),
            pltpu.VMEM((384, 384), BF16),
            pltpu.VMEM((384, 384), BF16),
            pltpu.VMEM((16, 24, 128), BF16),
            pltpu.VMEM((16, 24, 128), BF16),
            pltpu.VMEM((8, 8, 24, 128), BF16),
            pltpu.VMEM((64, 96, 128), BF16),
            pltpu.VMEM((2, 192, 3072), BF16),
            pltpu.VMEM((24, 128), F32),
            pltpu.VMEM((24, 128), F32),
            pltpu.VMEM((16, 24, 128), BF16),
            pltpu.VMEM((NY, BANDS, PW), BF16),
            pltpu.VMEM((NY, BANDS, PW), BF16),
            dma((8,)), dma((8,)), dma((16,)), dma((16,)), dma((8,)), dma((8,)), dma((2, 8)), dma((2, 8)),
            dma((8,)), dma((8,)), dma((2,)), dma, dma, dma((16,)), dma((16,)), dma((8,)), dma((8,)),
        ],
        compiler_params=pltpu.CompilerParams(
            collective_id=0, has_side_effects=True, vmem_limit_bytes=67043328 - 65536
        ),
    )(
        coeffs.T, miller, proj_atom.reshape(96, 128), species.reshape(1, ATOMS), positions, radial, coupling
    )
    return (coeffs.T.astype(F32) + change).astype(BF16).T


def solution(mesh):
    torus = Mesh(mesh.devices.reshape(NZ, NY, NC, NX), ("z", "y", "core", "band"))
    return jax.shard_map(
        shards,
        mesh=torus,
        in_specs=(P(GA, "band"), P(GA, "band"), P(None, GA), P(), P(), P(), P()),
        out_specs=P(GA, "band"),
        check_vma=False,
    )
```

time: 65.1 us -> 58.5 us (0.90)
  Pallas kernels: 62 us -> 56.9 us
  local copies, waits for them, and re-layouts: 2.77 us -> 0.01 us
  other arithmetic: 0.02 us -> 1.37 us
    pallas_call x1, Pallas kernels: 62 us -> 56.9 us  [shards(): pl.pallas_call(kernel, out_shape=jax.ShapeDtypeStruct((BANDS, PW), F32),...]
    unnamed x15 -> x2, local copies, waits for them, and re-layouts: 1.97 us -> 0.01 us
    transpose x0 -> x1, other arithmetic: none -> 1.37 us  [shards(): return (coeffs.T.astype(F32) + change).astype(BF16).T]
    convert_element_type x2 -> x0, local copies, waits for them, and re-layouts: 0.79 us -> none  [shards(): return (coeffs.astype(F32) + change).astype(BF16)]
where the time goes in v2:
time: 58.5 us; the launch traced here: 58.3 us
  Pallas kernels  56.9 us (97%)
  other arithmetic  1.37 us (2%)
    pallas_call x1, Pallas kernels, shards(): pl.pallas_call(kernel, out_shape=jax.ShapeDtypeStruct((BANDS, PW), F32),...  56.9 us
    transpose x1, other arithmetic, shards(): return (coeffs.T.astype(F32) + change).astype(BF16).T  1.37 us

profile of v2, /device:TPU:1, one launch (start us, length us, event | category | flops | bytes accessed | tf_op | source)
XLA Modules:
  0.0 58.3 jit_solution(8372964136615225244)
XLA Ops:
  0.0 0.0 copy-start
  0.0 56.9 %shard_map.73 = f32[32,256]{1,0:T(8,128)} custom-call(bf16[32,256]{1,0:T(8,128)(2,1)} %bitcast.6, s32[3,256]{1,0:T(4,128)} %miller_h.1, s32[96,128]{1,0:T(8,128)} %bitcast.7, s32[1,1024]{1,0:T(1,128)} %bitcast.8, f32[3,1024]{1,0:T(4,128)} %positions_h.1, f32[12,128]{1,0:T(8,128)} %radial_h.1, bf16[96,3072]{1,0:T(8,128)(2,1)} %coupling.1), custom_call_target="tpu_custom_call" | custom-call | tf_op jit(solution)/shard_map/pallas_call | solution.py:426
  56.9 0.0 copy-done
  56.9 1.4 %fusion = bf16[256,32]{0,1:T(8,128)(2,1)} fusion(f32[32,256]{1,0:T(8,128)} %shard_map.73, bf16[256,32]{0,1:T(8,128)(2,1)S(1)} %copy-done), kind=kLoop, calls=%fused_computation.1 | loop fusion | flops 24576 | bytes 65536 | tf_op jit(solution)/shard_map/transpose | solution.py:467
Async XLA Ops:
  0.0 56.9 %copy-start = (bf16[256,32]{0,1:T(8,128)(2,1)S(1)}, bf16[256,32]{0,1:T(8,128)(2,1)}, u32[]{:S(2)}) copy-start(bf16[256,32]{0,1:T(8,128)(2,1)} %param.7) | copy-start | bytes 49156

commit v3 on v2

--- a/solution.py
+++ b/solution.py
@@ -25,7 +25,8 @@
 FAR_FIRST = (4, 5, 3, 6, 2, 7, 1)
 NEAR_FIRST = (1, 7, 2, 6, 3, 5, 4)
 PLACE = {0: 0, 1: 1, 7: 2, 2: 3, 6: 4, 3: 5, 5: 6, 4: 7}
-BATCHES = ((0, 5), (5, 8))
+BATCHES = ((0, 1), (1, 3), (3, 5), (5, 8))
+BATCH_OF = (0, 1, 1, 2, 2, 3, 3, 3)
 F32 = jnp.float32
 BF16 = jnp.bfloat16
 
@@ -51,19 +52,17 @@
 
 
 SIN_TERMS = (
-    3.141592640130705,
-    -5.1677100835078935,
-    2.5500775232145623,
-    -0.5982912856196194,
-    0.07765766030331765,
+    3.141590270206989,
+    -5.167406733272336,
+    2.544010518503403,
+    -0.5594624554679108,
 )
 COS_TERMS = (
-    0.9999999997799042,
-    -4.934802137078829,
-    4.058709159556242,
-    -1.3352120030494103,
-    0.2349373138103021,
-    -0.024396324339225423,
+    0.9999999532476079,
+    -4.934792830619647,
+    4.058411352862676,
+    -1.3318765680812747,
+    0.21968961109860236,
 )
 
 
@@ -71,8 +70,7 @@
     r = turns - jnp.floor(turns + 0.5)
     y = r * r
     s = r * horner(y, SIN_TERMS)
-    c = horner(y, COS_TERMS)
-    return 1.0 - 2.0 * s * s, 2.0 * s * c
+    return 1.0 - 2.0 * (s * s), s * (horner(y, [t * (2.0 / MMAX) for t in COS_TERMS]))
 
 
 def fold(v):
@@ -126,46 +124,6 @@
     mtmp[...] = jnp.zeros_like(mtmp)
     mtmp[0:3, :] = miller[...].astype(F32)
     cbuf[y, 32:40, :] = mtmp[...].astype(BF16)
-
-    pl.semaphore_wait(barrier, greeted)
-
-    a_out = []
-    for d in NEAR_FIRST:
-        yy = (y + d) % NY
-        cp = remote(cbuf.at[y], cbuf.at[y], a_s.at[d], a_r.at[y], (z, yy, c, x))
-        cp.start()
-        a_out.append(cp)
-
-    side = x // 2
-
-    def half_of(xs, cs, h):
-        return ball.at[xs % 2, pl.ds(96 * cs + 48 * h, 48)], 4 * (xs % 2) + 2 * cs + h
-
-    b_out, own_copies, partner_copies = [], [], []
-    for first in range(2):
-        for way, dx in enumerate((1, 3)):
-            h = first if way == 0 else 1 - first
-            spot, sem = half_of(x, c, h)
-            cp = remote(
-                coupling.at[48 * h : 48 * (h + 1)], spot, b_s.at[2 * way + h], b_r.at[sem], (z, y, side, (x + dx) % NX)
-            )
-            cp.start()
-            b_out.append(cp)
-    for h in range(2):
-        spot, sem = half_of(x, c, h)
-        rows = coupling.at[48 * h : 48 * (h + 1)]
-        own_copies.append(pltpu.make_async_copy(rows, spot, b_l.at[h]))
-        partner_copies.append(remote(rows, spot, b_s.at[4 + h], b_r.at[sem], (z, y, 1 - c, x)))
-
-    @pl.when(side == c)
-    def _():
-        for cp in own_copies:
-            cp.start()
-
-    @pl.when(side != c)
-    def _():
-        for cp in partner_copies:
-            cp.start()
 
     def moved(natural, ours):
         atom_of = jnp.floor((natural.astype(F32) + 0.5) * (1.0 / NCH)).astype(jnp.int32)
@@ -202,6 +160,42 @@
     rad_top[128:256, :] = hi
     rad_low[...] = lo
 
+    pl.semaphore_wait(barrier, greeted)
+
+    for d in NEAR_FIRST:
+        yy = (y + d) % NY
+        remote(cbuf.at[y], cbuf.at[y], a_s, a_r.at[y], (z, yy, c, x)).start()
+
+    side = x // 2
+
+    def half_of(xs, cs, h):
+        return ball.at[xs % 2, pl.ds(96 * cs + 48 * h, 48)], 4 * (xs % 2) + 2 * cs + h
+
+    own_copies, partner_copies = [], []
+    for first in range(2):
+        for way, dx in enumerate((1, 3)):
+            h = first if way == 0 else 1 - first
+            spot, sem = half_of(x, c, h)
+            cp = remote(
+                coupling.at[48 * h : 48 * (h + 1)], spot, b_s.at[0], b_r.at[sem], (z, y, side, (x + dx) % NX)
+            )
+            cp.start()
+    for h in range(2):
+        spot, sem = half_of(x, c, h)
+        rows = coupling.at[48 * h : 48 * (h + 1)]
+        own_copies.append(pltpu.make_async_copy(rows, spot, b_l.at[h]))
+        partner_copies.append(remote(rows, spot, b_s.at[1], b_r.at[sem], (z, y, 1 - c, x)))
+
+    @pl.when(side == c)
+    def _():
+        for cp in own_copies:
+            cp.start()
+
+    @pl.when(side != c)
+    def _():
+        for cp in partner_copies:
+            cp.start()
+
     def make_block(yy, slot):
         m8 = cbuf[yy, 32:40, :].astype(F32)
         n2 = jnp.sum(m8 * m8, axis=0, keepdims=True)
@@ -214,25 +208,26 @@
             m0, m1, m2 = (jnp.broadcast_to(mt[rows, k : k + 1], (ROWS, 128)) for k in range(3))
             turns = m0 * place[0:1, :] + m1 * place[1:2, :] + m2 * place[2:3, :]
             cos, sin = circle(turns)
-            sin = sin * (1.0 / MMAX)
             phases = (cos, m0 * sin, m1 * sin, m2 * sin)
             for k in range(3):
                 amp = rad3[rows, 128 * k : 128 * (k + 1)]
                 for t in range(4):
                     ch = 4 * k + t
                     beta[slot, rows, 128 * ch : 128 * (ch + 1)] = (amp * phases[t]).astype(BF16)
+
+    def project(yy, slot):
         acc[...] += dot(cbuf[yy, 0:32, :], beta[slot])
 
     make_block(y, 7)
 
-    def step(k, carry):
-        d = jnp.where(k % 2 == 1, (k + 1) // 2, NY - k // 2)
+    last = (y, 7)
+    for k, d in enumerate(NEAR_FIRST):
         yy = (y + d) % NY
-        remote(cbuf.at[yy], cbuf.at[yy], a_s.at[0], a_r.at[yy], (z, y, c, x)).wait_recv()
-        make_block(yy, 7 - k)
-        return carry
-
-    lax.fori_loop(1, NY, step, 0)
+        remote(cbuf.at[yy], cbuf.at[yy], a_s, a_r.at[yy], (z, y, c, x)).wait_recv()
+        project(*last)
+        last = (yy, 6 - k)
+        make_block(*last)
+    project(*last)
 
     g32 = iota((32, 128), 1) >> 5
 
@@ -250,35 +245,31 @@
     ).T.astype(BF16)
     rs_send[...] = dot(perm[...], stacked).astype(BF16).reshape(16, 24, 128)
     sid = c * NZ + z
-    rs_out = []
     for d in FAR_FIRST:
         for o in range(NC):
             zz, cc = (z + d) % NZ, (c + o) % NC
-            cp = remote(rs_send.at[cc * NZ + zz], rs_recv.at[sid], rs_s.at[d * 2 + o], rs_r.at[sid], (zz, y, cc, x))
-            cp.start()
-            rs_out.append(cp)
-    cp = remote(rs_send.at[(1 - c) * NZ + z], rs_recv.at[sid], rs_s.at[1], rs_r.at[sid], (z, y, 1 - c, x))
-    cp.start()
-    rs_out.append(cp)
+            remote(rs_send.at[cc * NZ + zz], rs_recv.at[sid], rs_s, rs_r, (zz, y, cc, x)).start()
+    remote(rs_send.at[(1 - c) * NZ + z], rs_recv.at[sid], rs_s, rs_r, (z, y, 1 - c, x)).start()
 
     near = 2 * c + 1 - x % 2
     which = jnp.where((near + 1) % NX == x, 0, 1)
     for cs in range(2):
         spot, sem = half_of(near, cs, which)
         remote(spot, spot, b_s.at[0], b_r.at[sem], (z, y, c, x)).wait_recv()
-        cp = remote(spot, spot, b_s.at[6 + cs], b_r.at[sem], (z, y, c, (near + 2) % NX))
-        cp.start()
-        b_out.append(cp)
-
-    def wait16(buf, sems, s):
-        remote(buf.at[s], buf.at[s], rs_s.at[0], sems.at[s], (z, y, c, x)).wait_recv()
-
+        remote(spot, spot, b_s.at[2], b_r.at[sem], (z, y, c, (near + 2) % NX)).start()
+
+    def received(buf, sem):
+        remote(buf, buf, rs_s, sem, (z, y, c, x)).wait_recv()
+
+    def sent(buf, sem):
+        remote(buf, buf, sem, rs_r, (z, y, c, x)).wait_send()
+
+    received(rs_recv.at[0:15], rs_r)
     total = rs_send[sid].astype(F32)
-    order16 = [(0, 1)] + [(d, o) for d in NEAR_FIRST for o in range(NC)]
-    for d, o in order16:
-        s = ((c + o) % NC) * NZ + (z + d) % NZ
-        wait16(rs_recv, rs_r, s)
-        total = total + rs_recv[s].astype(F32)
+    for d in range(NZ):
+        for o in range(NC):
+            if d or o:
+                total = total + rs_recv[((c + o) % NC) * NZ + (z + d) % NZ].astype(F32)
 
     fm = z + c * (y - z)
     sm = y + c * (z - y)
@@ -290,27 +281,22 @@
         return (z + c * (s - z), y + (1 - c) * (s - y), c, x)
 
     nbuf[sm, 0] = total.astype(BF16)
-    g_out = []
     for d in FAR_FIRST:
         k = PLACE[(8 - d) % 8]
-        cp = remote(nbuf.at[sm, 0], nbuf.at[sm, k], g1_s.at[d], g1_r.at[k], at_first((fm + d) % 8))
-        cp.start()
-        g_out.append(cp)
+        remote(nbuf.at[sm, 0], nbuf.at[sm, k], g1_s, g1_r.at[BATCH_OF[k]], at_first((fm + d) % 8)).start()
     for batch, (low, high) in enumerate(BATCHES):
-        for k in range(max(low, 1), high):
-            remote(nbuf.at[sm, k], nbuf.at[sm, k], g1_s.at[0], g1_r.at[k], (z, y, c, x)).wait_recv()
+        if batch:
+            received(nbuf.at[sm, low:high], g1_r.at[batch])
         rows = nbuf.at[sm, low:high]
         for d in FAR_FIRST:
-            cp = remote(rows, rows, g2_s.at[batch, d], g2_r.at[batch, sm], at_second((sm + d) % 8))
-            cp.start()
-            g_out.append(cp)
+            remote(rows, rows, g2_s, g2_r.at[sm], at_second((sm + d) % 8)).start()
 
     group = iota((24, 128), 1) >> 5
 
     masks = [(group == j).astype(F32).astype(BF16) for j in range(4)]
 
-    def spread_rows(s, low, high):
-        for k in range(low, high):
+    def spread_row(s):
+        for k in range(8):
             f = (fm + ((k + 1) // 2 if k % 2 else 8 - k // 2)) % 8
             zz = f + c * (s - f)
             yy = s + c * (f - s)
@@ -319,13 +305,11 @@
             for j in range(4):
                 wide[n, 24 * j : 24 * (j + 1), :] = piece * masks[j]
 
-    spread_rows(sm, 0, 8)
-    for batch, (low, high) in enumerate(BATCHES):
-        for d in NEAR_FIRST:
-            ss = (sm + d) % 8
-            rows = nbuf.at[ss, low:high]
-            remote(rows, rows, g1_s.at[0], g2_r.at[batch, ss], (z, y, c, x)).wait_recv()
-            spread_rows(ss, low, high)
+    spread_row(sm)
+    for d in NEAR_FIRST:
+        ss = (sm + d) % 8
+        received(nbuf.at[ss], g2_r.at[ss])
+        spread_row(ss)
 
     for xh in range(2):
         for cs in range(2):
@@ -343,36 +327,31 @@
                 def _():
                     remote(spot, spot, b_s.at[0], b_r.at[sem], (z, y, c, x)).wait_recv()
 
-    part = jnp.zeros((192, 128), F32)
-    for xh in range(2):
-        part = part + dot(ball[xh], wide[32 * xh : 32 * (xh + 1)].reshape(3072, 128))
-    part = fold(part)
-    packs = []
-    for r in range(2):
-        pack = jnp.zeros((24, 128), F32)
-        for k in range(4):
-            pack = jnp.where(group == k, part[96 * r + 24 * k : 96 * r + 24 * (k + 1)], pack)
-        packs.append(pack)
-    xsend[...] = jnp.where(c == 0, packs[1], packs[0])
+    def product(r):
+        rows = pl.ds(pl.multiple_of(96 * r, 32), 96)
+        part = jnp.zeros((96, 128), F32)
+        for xh in range(2):
+            part = part + dot(ball[xh, rows], wide[32 * xh : 32 * (xh + 1)].reshape(3072, 128))
+        part = fold(part)
+        pack = part[0:24]
+        for k in range(1, 4):
+            pack = jnp.where(group == k, part[24 * k : 24 * (k + 1)], pack)
+        return pack
+
+    xsend[...] = product(1 - c)
     xcp = remote(xsend, xrecv, x_s, x_r, (z, y, 1 - c, x))
     xcp.start()
-    own = jnp.where(c == 0, packs[0], packs[1])
+    own = product(c)
     xcp.wait()
     qm = 2 * z + c
     mx[qm] = (own + xrecv[...]).astype(BF16)
 
-    e_out = []
     for d in FAR_FIRST:
         for o in range(NC):
             zz, cc = (z + d) % NZ, (c + o) % NC
-            cp = remote(mx.at[qm], mx.at[qm], e_s.at[d * 2 + o], e_r.at[qm], (zz, y, cc, x))
-            cp.start()
-            e_out.append(cp)
-    cp = remote(mx.at[qm], mx.at[qm], e_s.at[1], e_r.at[qm], (z, y, 1 - c, x))
-    cp.start()
-    e_out.append(cp)
-    for d, o in order16:
-        wait16(mx, e_r, 2 * ((z + d) % NZ) + (c + o) % NC)
+            remote(mx.at[qm], mx.at[qm], e_s, e_r, (zz, y, cc, x)).start()
+    remote(mx.at[qm], mx.at[qm], e_s, e_r, (z, y, 1 - c, x)).start()
+    received(mx.at[0:15], e_r)
 
     ours = dot(back[...], mx[...].reshape(384, 128))
     ours = ours.T
@@ -388,7 +367,6 @@
 
     lhs = jnp.concatenate([channel(k) for k in range(NCH)], axis=1).astype(BF16)
 
-    f_out = []
     for pair in range(4):
         both = lax.dot_general(
             lhs, beta[2 * pair : 2 * pair + 2].reshape(2 * PW, WIDTH),
@@ -402,27 +380,32 @@
             d = FAR_FIRST[slot]
             yy = (y + d) % NY
             fsend[slot] = total.astype(BF16)
-            cp = remote(fsend.at[slot], frecv.at[y], f_s.at[d], f_r.at[y], (z, yy, c, x))
-            cp.start()
-            f_out.append(cp)
+            remote(fsend.at[slot], frecv.at[y], f_s, f_r, (z, yy, c, x)).start()
+    received(frecv.at[0:7], f_r)
     for d in NEAR_FIRST:
-        yy = (y + d) % NY
-        remote(frecv.at[yy], frecv.at[yy], f_s.at[0], f_r.at[yy], (z, y, c, x)).wait_recv()
-        total = total + frecv[yy].astype(F32)
+        total = total + frecv[(y + d) % NY].astype(F32)
     out[...] = total
 
-    for cp in a_out + b_out + rs_out + g_out + e_out + f_out:
-        cp.wait_send()
+    sent(cbuf.at[0:7], a_s)
+    sent(ball.at[0], b_s.at[0])
+    sent(ball.at[0, 0:96], b_s.at[2])
+    sent(rs_send.at[0:15], rs_s)
+    sent(nbuf.at[0, 0:7], g1_s)
+    sent(nbuf.at[0:7], g2_s)
+    sent(mx.at[0:15], e_s)
+    sent(fsend.at[0:7], f_s)
 
     @pl.when(side != c)
     def _():
-        for cp in partner_copies:
-            cp.wait_send()
+        sent(ball.at[0, 0:96], b_s.at[1])
 
 
 def shards(coeffs, coupling, miller, species, proj_atom, positions, radial):
     vmem = pl.BlockSpec(memory_space=pltpu.VMEM)
     dma = pltpu.SemaphoreType.DMA
+    inputs = (
+        coeffs.T, miller, proj_atom.reshape(96, 128), species.reshape(1, ATOMS), positions, radial, coupling
+    )
     change = pl.pallas_call(
         kernel,
         out_shape=jax.ShapeDtypeStruct((BANDS, PW), F32),
@@ -455,14 +438,14 @@
             pltpu.VMEM((16, 24, 128), BF16),
             pltpu.VMEM((NY, BANDS, PW), BF16),
             pltpu.VMEM((NY, BANDS, PW), BF16),
-            dma((8,)), dma((8,)), dma((16,)), dma((16,)), dma((8,)), dma((8,)), dma((2, 8)), dma((2, 8)),
-            dma((8,)), dma((8,)), dma((2,)), dma, dma, dma((16,)), dma((16,)), dma((8,)), dma((8,)),
+            dma, dma((8,)), dma, dma, dma, dma((4,)), dma, dma((8,)),
+            dma((3,)), dma((8,)), dma((2,)), dma, dma, dma, dma, dma, dma,
         ],
         compiler_params=pltpu.CompilerParams(
-            collective_id=0, has_side_effects=True, vmem_limit_bytes=67043328 - 65536
+            collective_id=0, has_side_effects=True, vmem_limit_bytes=48 * 1024 * 1024
         ),
     )(
-        coeffs.T, miller, proj_atom.reshape(96, 128), species.reshape(1, ATOMS), positions, radial, coupling
+        *(pltpu.with_memory_space_constraint(v, pltpu.HBM) for v in inputs)
     )
     return (coeffs.T.astype(F32) + change).astype(BF16).T
 

time: 58.5 us -> 53.6 us (0.916)
  Pallas kernels: 56.9 us -> 52.7 us
  other arithmetic: 1.37 us -> 0.61 us
    pallas_call x1, Pallas kernels: 56.9 us -> 52.7 us  [shards(): pl.pallas_call(kernel, out_shape=jax.ShapeDtypeStruct((BANDS, PW), F32),...]
    transpose x1, other arithmetic: 1.37 us -> 0.61 us  [shards(): return (coeffs.T.astype(F32) + change).astype(BF16).T]
where the time goes in v3:
time: 53.6 us; the launch traced here: 53.4 us
  Pallas kernels  52.7 us (98%)
  other arithmetic  0.61 us (1%)
    pallas_call x1, Pallas kernels, shards(): pl.pallas_call(kernel, out_shape=jax.ShapeDtypeStruct((BANDS, PW), F32),...  52.7 us

profile of v3, /device:TPU:1, one launch (start us, length us, event | category | flops | bytes accessed | tf_op | source)
XLA Modules:
  0.0 53.4 jit_solution(5429038237872713056)
XLA Ops:
  0.0 0.0 copy-start
  0.0 52.7 %shard_map.73 = f32[32,256]{1,0:T(8,128)S(1)} custom-call(bf16[32,256]{1,0:T(8,128)(2,1)} %bitcast.6, s32[3,256]{1,0:T(4,128)} %miller_h.1, s32[96,128]{1,0:T(8,128)} %bitcast.7, s32[1,1024]{1,0:T(1,128)} %bitcast.8, f32[3,1024]{1,0:T(4,128)} %positions_h.1, f32[12,128]{1,0:T(8,128)} %radial_h.1, bf16[96,3072]{1,0:T(8,128)(2,1)} %coupling.1), custom_call_target="tpu_custom_call" | custom-call | tf_op jit(solution)/shard_map/pallas_call | solution.py:409
  52.8 0.0 copy-done
  52.8 0.6 %fusion = bf16[256,32]{0,1:T(8,128)(2,1)} fusion(f32[32,256]{1,0:T(8,128)S(1)} %shard_map.73, bf16[256,32]{0,1:T(8,128)(2,1)S(1)} %copy-done), kind=kLoop, calls=%fused_computation.1 | loop fusion | flops 24576 | bytes 65536 | tf_op jit(solution)/shard_map/transpose | solution.py:450
Async XLA Ops:
  0.0 52.8 %copy-start = (bf16[256,32]{0,1:T(8,128)(2,1)S(1)}, bf16[256,32]{0,1:T(8,128)(2,1)}, u32[]{:S(2)}) copy-start(bf16[256,32]{0,1:T(8,128)(2,1)} %param.7) | copy-start | bytes 49156

commit v4 on v3

--- a/solution.py
+++ b/solution.py
@@ -22,6 +22,8 @@
 HALF = 6144
 SCALE = 1.0 / math.sqrt(32768.0)
 MESH = pl.DeviceIdType.MESH
+LAG = 2
+GROUPS = ((0, 1), (1, 2), (2, 4), (4, 6), (6, 8))
 FAR_FIRST = (4, 5, 3, 6, 2, 7, 1)
 NEAR_FIRST = (1, 7, 2, 6, 3, 5, 4)
 PLACE = {0: 0, 1: 1, 7: 2, 2: 3, 6: 4, 3: 5, 5: 6, 4: 7}
@@ -80,9 +82,9 @@
 
 def kernel(
     coeffs_h, miller_h, owner_h, species_h, positions_h, radial_h, coupling, out,
-    miller, owner, species, positions, radial, in_s, cbuf, mtmp, beta, acc, place, rad3, rad_top, rad_low, perm, back,
+    miller, owner, species, positions, radial, in_s, cbuf, mbuf, mtmp, beta, acc, place, rad3, rad_top, perm, back,
     rs_send, rs_recv, nbuf, wide, ball, xsend, xrecv, mx, fsend, frecv,
-    a_s, a_r, rs_s, rs_r, g1_s, g1_r, g2_s, g2_r, b_s, b_r, b_l, x_s, x_r, e_s, e_r, f_s, f_r,
+    m_s, m_r, a_s, a_r, rs_s, rs_r, g1_s, g1_r, g2_s, g2_r, b_s, b_r, b_l, x_s, x_r, e_s, e_r, f_s, f_r,
 ):
     z, y, c, x = (lax.axis_index(a) for a in ("z", "y", "core", "band"))
     barrier = pltpu.get_barrier_semaphore()
@@ -91,7 +93,7 @@
         pltpu.make_async_copy(src, dst, in_s.at[k])
         for k, (src, dst) in enumerate(
             (
-                (miller_h, miller), (coeffs_h, cbuf.at[y, 0:32]), (owner_h, owner),
+                (miller_h, miller), (coeffs_h, cbuf.at[y]), (owner_h, owner),
                 (radial_h, radial), (positions_h, positions), (species_h, species),
             )
         )
@@ -118,13 +120,6 @@
         )
     for cp in loads[2:]:
         cp.start()
-    for cp in loads[:2]:
-        cp.wait()
-
-    mtmp[...] = jnp.zeros_like(mtmp)
-    mtmp[0:3, :] = miller[...].astype(F32)
-    cbuf[y, 32:40, :] = mtmp[...].astype(BF16)
-
     def moved(natural, ours):
         atom_of = jnp.floor((natural.astype(F32) + 0.5) * (1.0 / NCH)).astype(jnp.int32)
         return (ours == (natural - NCH * atom_of) * 32 + atom_of).astype(F32).astype(BF16)
@@ -133,6 +128,13 @@
     perm[...] = moved(iota(square, 0), iota(square, 1))
     back[...] = moved(iota(square, 1), iota(square, 0))
     acc[...] = jnp.zeros_like(acc)
+
+    for cp in loads[:2]:
+        cp.wait()
+
+    mtmp[...] = jnp.zeros_like(mtmp)
+    mtmp[0:3, :] = miller[...].astype(F32)
+    mbuf[y] = mtmp[...].astype(BF16)
 
     for cp in loads[2:]:
         cp.wait()
@@ -158,10 +160,12 @@
     hi, lo = split2(dot(rad, pick_s, precision=lax.Precision.HIGHEST))
     rad_top[0:128, :] = hi
     rad_top[128:256, :] = hi
-    rad_low[...] = lo
+    rad_top[256:384, :] = lo
 
     pl.semaphore_wait(barrier, greeted)
 
+    for d in NEAR_FIRST:
+        remote(mbuf.at[y], mbuf.at[y], m_s, m_r.at[y], (z, (y + d) % NY, c, x)).start()
     for d in NEAR_FIRST:
         yy = (y + d) % NY
         remote(cbuf.at[y], cbuf.at[y], a_s, a_r.at[y], (z, yy, c, x)).start()
@@ -197,13 +201,13 @@
             cp.start()
 
     def make_block(yy, slot):
-        m8 = cbuf[yy, 32:40, :].astype(F32)
+        m8 = mbuf[yy].astype(F32)
         n2 = jnp.sum(m8 * m8, axis=0, keepdims=True)
         qv = n2 * ((QBINS - 1) / (3.0 * MMAX * MMAX))
         mt = jnp.where(iota((8, PW), 0) == 3, qv, m8).T
         hats = jnp.maximum(0.0, 1.0 - jnp.abs(mt[:, 3:4] - iota((PW, 128), 1).astype(F32)))
         h_hi, h_lo = split2(hats)
-        rad3[...] = dot(jnp.concatenate([h_hi, h_lo], axis=1), rad_top[...]) + dot(h_hi, rad_low[...])
+        rad3[...] = dot(jnp.concatenate([h_hi, h_lo, h_hi], axis=1), rad_top[...])
         for rows in (slice(r, r + ROWS) for r in range(0, PW, ROWS)):
             m0, m1, m2 = (jnp.broadcast_to(mt[rows, k : k + 1], (ROWS, 128)) for k in range(3))
             turns = m0 * place[0:1, :] + m1 * place[1:2, :] + m2 * place[2:3, :]
@@ -216,18 +220,26 @@
                     beta[slot, rows, 128 * ch : 128 * (ch + 1)] = (amp * phases[t]).astype(BF16)
 
     def project(yy, slot):
-        acc[...] += dot(cbuf[yy, 0:32, :], beta[slot])
+        acc[...] += dot(cbuf[yy], beta[slot])
 
     make_block(y, 7)
 
-    last = (y, 7)
-    for k, d in enumerate(NEAR_FIRST):
-        yy = (y + d) % NY
-        remote(cbuf.at[yy], cbuf.at[yy], a_s, a_r.at[yy], (z, y, c, x)).wait_recv()
-        project(*last)
-        last = (yy, 6 - k)
-        make_block(*last)
-    project(*last)
+    blocks = [(y, 7)] + [((y + d) % NY, 6 - k) for k, d in enumerate(NEAR_FIRST)]
+
+    def gathered(k):
+        yy, slot = blocks[k]
+        if k:
+            remote(cbuf.at[yy], cbuf.at[yy], a_s, a_r.at[yy], (z, y, c, x)).wait_recv()
+        project(yy, slot)
+
+    for k in range(1, NY):
+        yy, slot = blocks[k]
+        remote(mbuf.at[yy], mbuf.at[yy], m_s, m_r.at[yy], (z, y, c, x)).wait_recv()
+        if k >= LAG:
+            gathered(k - LAG)
+        make_block(yy, slot)
+    for k in range(NY - LAG, NY):
+        gathered(k)
 
     g32 = iota((32, 128), 1) >> 5
 
@@ -367,14 +379,13 @@
 
     lhs = jnp.concatenate([channel(k) for k in range(NCH)], axis=1).astype(BF16)
 
-    for pair in range(4):
+    for low, high in GROUPS:
         both = lax.dot_general(
-            lhs, beta[2 * pair : 2 * pair + 2].reshape(2 * PW, WIDTH),
+            lhs, beta[low:high].reshape((high - low) * PW, WIDTH),
             (((1,), (1,)), ((), ())), preferred_element_type=F32,
         )
-        for half in range(2):
-            total = both[:, PW * half : PW * (half + 1)]
-            slot = 2 * pair + half
+        for slot in range(low, high):
+            total = both[:, PW * (slot - low) : PW * (slot - low + 1)]
             if slot == 7:
                 break
             d = FAR_FIRST[slot]
@@ -387,6 +398,7 @@
     out[...] = total
 
     sent(cbuf.at[0:7], a_s)
+    sent(mbuf.at[0:7], m_s)
     sent(ball.at[0], b_s.at[0])
     sent(ball.at[0, 0:96], b_s.at[2])
     sent(rs_send.at[0:15], rs_s)
@@ -418,14 +430,14 @@
             pltpu.VMEM((3, ATOMS), F32),
             pltpu.VMEM((12, QBINS), F32),
             dma((6,)),
-            pltpu.VMEM((NY, 40, PW), BF16),
+            pltpu.VMEM((NY, BANDS, PW), BF16),
+            pltpu.VMEM((NY, 8, PW), BF16),
             pltpu.VMEM((8, PW), F32),
             pltpu.VMEM((NY, PW, WIDTH), BF16),
             pltpu.VMEM((BANDS, WIDTH), F32),
             pltpu.VMEM((3, 128), F32),
             pltpu.VMEM((PW, 384), F32),
-            pltpu.VMEM((256, 384), BF16),
-            pltpu.VMEM((128, 384), BF16),
+            pltpu.VMEM((384, 384), BF16),
             pltpu.VMEM((384, 384), BF16),
             pltpu.VMEM((384, 384), BF16),
             pltpu.VMEM((16, 24, 128), BF16),
@@ -438,7 +450,7 @@
             pltpu.VMEM((16, 24, 128), BF16),
             pltpu.VMEM((NY, BANDS, PW), BF16),
             pltpu.VMEM((NY, BANDS, PW), BF16),
-            dma, dma((8,)), dma, dma, dma, dma((4,)), dma, dma((8,)),
+            dma, dma((8,)), dma, dma((8,)), dma, dma, dma, dma((4,)), dma, dma((8,)),
             dma((3,)), dma((8,)), dma((2,)), dma, dma, dma, dma, dma, dma,
         ],
         compiler_params=pltpu.CompilerParams(

time: 53.6 us -> 53.8 us (level)
  no operation moved by 1% of the time
where the time goes in v4:
time: 53.8 us; the launch traced here: 53.6 us
  Pallas kernels  52.9 us (98%)
  other arithmetic  0.61 us (1%)
    pallas_call x1, Pallas kernels, shards(): pl.pallas_call(kernel, out_shape=jax.ShapeDtypeStruct((BANDS, PW), F32),...  52.9 us

profile of v4, /device:TPU:1, one launch (start us, length us, event | category | flops | bytes accessed | tf_op | source)
XLA Modules:
  0.0 53.6 jit_solution(13290503537051864077)
XLA Ops:
  0.0 0.0 copy-start
  0.0 52.9 %shard_map.73 = f32[32,256]{1,0:T(8,128)S(1)} custom-call(bf16[32,256]{1,0:T(8,128)(2,1)} %bitcast.6, s32[3,256]{1,0:T(4,128)} %miller_h.1, s32[96,128]{1,0:T(8,128)} %bitcast.7, s32[1,1024]{1,0:T(1,128)} %bitcast.8, f32[3,1024]{1,0:T(4,128)} %positions_h.1, f32[12,128]{1,0:T(8,128)} %radial_h.1, bf16[96,3072]{1,0:T(8,128)(2,1)} %coupling.1), custom_call_target="tpu_custom_call" | custom-call | tf_op jit(solution)/shard_map/pallas_call | solution.py:421
  52.9 0.0 copy-done
  53.0 0.6 %fusion = bf16[256,32]{0,1:T(8,128)(2,1)} fusion(f32[32,256]{1,0:T(8,128)S(1)} %shard_map.73, bf16[256,32]{0,1:T(8,128)(2,1)S(1)} %copy-done), kind=kLoop, calls=%fused_computation.1 | loop fusion | flops 24576 | bytes 65536 | tf_op jit(solution)/shard_map/transpose | solution.py:462
Async XLA Ops:
  0.0 52.9 %copy-start = (bf16[256,32]{0,1:T(8,128)(2,1)S(1)}, bf16[256,32]{0,1:T(8,128)(2,1)}, u32[]{:S(2)}) copy-start(bf16[256,32]{0,1:T(8,128)(2,1)} %param.7) | copy-start | bytes 49156

commit v5 on v3

--- a/solution.py
+++ b/solution.py
@@ -118,13 +118,6 @@
         )
     for cp in loads[2:]:
         cp.start()
-    for cp in loads[:2]:
-        cp.wait()
-
-    mtmp[...] = jnp.zeros_like(mtmp)
-    mtmp[0:3, :] = miller[...].astype(F32)
-    cbuf[y, 32:40, :] = mtmp[...].astype(BF16)
-
     def moved(natural, ours):
         atom_of = jnp.floor((natural.astype(F32) + 0.5) * (1.0 / NCH)).astype(jnp.int32)
         return (ours == (natural - NCH * atom_of) * 32 + atom_of).astype(F32).astype(BF16)
@@ -133,6 +126,13 @@
     perm[...] = moved(iota(square, 0), iota(square, 1))
     back[...] = moved(iota(square, 1), iota(square, 0))
     acc[...] = jnp.zeros_like(acc)
+
+    for cp in loads[:2]:
+        cp.wait()
+
+    mtmp[...] = jnp.zeros_like(mtmp)
+    mtmp[0:3, :] = miller[...].astype(F32)
+    cbuf[y, 32:40, :] = mtmp[...].astype(BF16)
 
     for cp in loads[2:]:
         cp.wait()

time: 53.6 us -> 53.7 us (level)
  no operation moved by 1% of the time
where the time goes in v5:
time: 53.7 us; the launch traced here: 53.5 us
  Pallas kernels  52.8 us (98%)
  other arithmetic  0.61 us (1%)
    pallas_call x1, Pallas kernels, shards(): pl.pallas_call(kernel, out_shape=jax.ShapeDtypeStruct((BANDS, PW), F32),...  52.8 us

profile of v5, /device:TPU:1, one launch (start us, length us, event | category | flops | bytes accessed | tf_op | source)
XLA Modules:
  0.0 53.5 jit_solution(15311199220284990468)
XLA Ops:
  0.0 0.0 copy-start
  0.0 52.8 %shard_map.73 = f32[32,256]{1,0:T(8,128)S(1)} custom-call(bf16[32,256]{1,0:T(8,128)(2,1)} %bitcast.6, s32[3,256]{1,0:T(4,128)} %miller_h.1, s32[96,128]{1,0:T(8,128)} %bitcast.7, s32[1,1024]{1,0:T(1,128)} %bitcast.8, f32[3,1024]{1,0:T(4,128)} %positions_h.1, f32[12,128]{1,0:T(8,128)} %radial_h.1, bf16[96,3072]{1,0:T(8,128)(2,1)} %coupling.1), custom_call_target="tpu_custom_call" | custom-call | tf_op jit(solution)/shard_map/pallas_call | solution.py:409
  52.8 0.0 copy-done
  52.8 0.6 %fusion = bf16[256,32]{0,1:T(8,128)(2,1)} fusion(f32[32,256]{1,0:T(8,128)S(1)} %shard_map.73, bf16[256,32]{0,1:T(8,128)(2,1)S(1)} %copy-done), kind=kLoop, calls=%fused_computation.1 | loop fusion | flops 24576 | bytes 65536 | tf_op jit(solution)/shard_map/transpose | solution.py:450
Async XLA Ops:
  0.0 52.8 %copy-start = (bf16[256,32]{0,1:T(8,128)(2,1)S(1)}, bf16[256,32]{0,1:T(8,128)(2,1)}, u32[]{:S(2)}) copy-start(bf16[256,32]{0,1:T(8,128)(2,1)} %param.7) | copy-start | bytes 49156
